TPU v7x, 256 devices: a whole 4x4x8 slice. The times are simulated.
256 devices in a mesh: frame: 64 (over x, z, y_lo), row: 4 (over y_hi, core).
Axes of the slice: x: 4, y: 4 (y_hi: 2, y_lo: 2; y = y_hi * 2 + y_lo), z: 8, core: 2. Of those that a mesh axis runs over, the one named last changes fastest.
Arguments:
- clip: bfloat16 [128, 16, 256, 128], P('frame', 'row'), may hold values from -6 to 6
- first_kernel: bfloat16 [3, 3, 3, 128, 128], replicated, may hold values from -0.109375 to 0.109375
- second_kernel: bfloat16 [3, 3, 3, 128, 128], replicated, may hold values from -0.109375 to 0.109375
- cotangent: bfloat16 [128, 16, 256, 128], P('frame', 'row'), may hold values from -6 to 6
Outputs:
- critic_map: bfloat16 [128, 16, 256, 128], P('frame', 'row')
- clip_grad: bfloat16 [128, 16, 256, 128], P('frame', 'row')
- first_grad: float32 [3, 3, 3, 128, 128], replicated
- second_grad: float32 [3, 3, 3, 128, 128], replicated
All inputs are finite; a program needn't handle non-finite values.
Results may differ from a plain program's by a relative error of at most 0.012.
Values may be sent and summed in bfloat16 or wider, within the bound.
A program may use at most 64 MiB of HBM per device.

v0:
```python
import functools

import jax
import jax.numpy as jnp
from jax import lax
from jax.experimental import pallas as pl
from jax.experimental.pallas import tpu as pltpu
from jax.sharding import PartitionSpec as P

MESH = pl.DeviceIdType.MESH
BF16, F32 = jnp.bfloat16, jnp.float32
CH = 128

NX, NY, NZ = 4, 4, 8
NXY = NX * NY
BLK = 112
HALF = NXY * BLK
ROWS = 2 * HALF
TILE = 16
ZT = BLK // TILE


class Place:
    def __init__(self):
        f, r = lax.axis_index("frame"), lax.axis_index("row")
        self.x, self.z = f // (2 * NZ), (f // 2) % NZ
        self.y, self.core = (r // 2) * 2 + f % 2, r % 2
        self.p = self.x * NY + self.y

    @staticmethod
    def at(x, y, z, core):
        return ((x * NZ + z) * 2 + y % 2, (y // 2) * 2 + core)


def remote(src, dst, send, recv, device):
    return pltpu.make_async_remote_copy(
        src_ref=src, dst_ref=dst, send_sem=send, recv_sem=recv, device_id=device, device_id_type=MESH)


def take(ref, rows, sem):
    view = ref.at[pl.ds(0, rows)]
    pltpu.make_async_copy(view, view, sem).wait()


def rows_of(start, size):
    return pl.ds(pl.multiple_of(start, TILE), size)


class AllReduce:
    def __init__(self, me, part, full, other, slots, piece, tiles, send, recv):
        self.me, self.part, self.full = me, part, full
        self.other, self.slots, self.piece, self.tiles = other, slots, piece, tiles
        self.send, self.recv = send, recv

    def xy_peer(self, o):
        p = (self.me.p + o) % NXY
        return p, Place.at(p // NY, p % NY, self.me.z, self.me.core)

    def z_peer(self, o):
        d = (self.me.z + o) % NZ
        return d, Place.at(self.me.x, self.me.y, d, self.me.core)

    def twin(self):
        return Place.at(self.me.x, self.me.y, self.me.z, 1 - self.me.core)

    def scatter_core(self):
        remote(self.part.at[rows_of((1 - self.me.core) * HALF, HALF)], self.other,
               self.send.at[0], self.recv.at[0], self.twin()).start()

    def scatter_xy(self):
        me = self.me
        take(self.other, HALF, self.recv.at[0])
        base = me.core * HALF

        @pl.loop(0, HALF // 128)
        def _(i):
            mine = rows_of(base + i * 128, 128)
            total = self.part[mine, :].astype(jnp.float32) + self.other[rows_of(i * 128, 128), :].astype(jnp.float32)
            self.part[mine, :] = total.astype(jnp.bfloat16)

        @pl.loop(1, NXY)
        def _(o):
            p, peer = self.xy_peer(o)
            remote(self.part.at[rows_of(base + p * BLK, BLK)], self.slots.at[rows_of(me.p * BLK, BLK)],
                   self.send.at[1], self.recv.at[1], peer).start()

    def scatter_z(self):
        me = self.me
        take(self.slots, (NXY - 1) * BLK, self.recv.at[1])
        total = self.part[rows_of(me.core * HALF + me.p * BLK, BLK), :].astype(jnp.float32)

        def add(o, total):
            p = (me.p + o) % NXY
            return total + self.slots[rows_of(p * BLK, BLK), :].astype(jnp.float32)

        self.piece[...] = lax.fori_loop(1, NXY, add, total).astype(jnp.bfloat16)

        @pl.loop(1, NZ)
        def _(o):
            d, peer = self.z_peer(o)

            @pl.when(d < ZT)
            def _():
                remote(self.piece.at[rows_of(d * TILE, TILE)], self.tiles.at[rows_of(me.z * TILE, TILE)],
                       self.send.at[2], self.recv.at[2], peer).start()

    def gather_z(self):
        me = self.me

        @pl.when(me.z < ZT)
        def _():
            take(self.tiles, (NZ - 1) * TILE, self.recv.at[2])
            total = self.piece[rows_of(me.z * TILE, TILE), :].astype(jnp.float32)
            for o in range(1, NZ):
                d = (me.z + o) % NZ
                total = total + self.tiles[rows_of(d * TILE, TILE), :].astype(jnp.float32)
            mine = rows_of(me.core * HALF + me.p * BLK + me.z * TILE, TILE)
            self.full[mine, :] = total.astype(jnp.bfloat16)

            @pl.loop(1, NZ)
            def _(o):
                d, peer = self.z_peer(o)
                remote(self.full.at[mine], self.full.at[mine], self.send.at[3], self.recv.at[3], peer).start()

    def gather_xy(self):
        me = self.me

        @pl.when(me.z < ZT)
        def _():
            take(self.full, (ZT - 1) * TILE, self.recv.at[3])

        @pl.when(me.z >= ZT)
        def _():
            take(self.full, ZT * TILE, self.recv.at[3])

        mine = rows_of(me.core * HALF + me.p * BLK, BLK)

        @pl.loop(1, NXY)
        def _(o):
            p, peer = self.xy_peer(o)
            remote(self.full.at[mine], self.full.at[mine], self.send.at[4], self.recv.at[4], peer).start()

    def gather_core(self):
        take(self.full, (NXY - 1) * BLK, self.recv.at[4])
        mine = rows_of(self.me.core * HALF, HALF)
        remote(self.full.at[mine], self.full.at[mine], self.send.at[5], self.recv.at[5], self.twin()).start()

    def finish(self):
        me = self.me
        take(self.full, HALF, self.recv.at[5])
        take(self.part, HALF, self.send.at[0])
        take(self.part, (NXY - 1) * BLK, self.send.at[1])

        @pl.when(me.z < ZT)
        def _():
            take(self.piece, (ZT - 1) * TILE, self.send.at[2])
            take(self.full, (NZ - 1) * TILE, self.send.at[3])

        @pl.when(me.z >= ZT)
        def _():
            take(self.piece, ZT * TILE, self.send.at[2])

        take(self.full, (NXY - 1) * BLK, self.send.at[4])
        take(self.full, HALF, self.send.at[5])


def greet_reduce_peers(me, barrier):
    pl.semaphore_signal(barrier, inc=1, device_id=Place.at(me.x, me.y, me.z, 1 - me.core), device_id_type=MESH)

    @pl.loop(1, NXY)
    def _(o):
        p = (me.p + o) % NXY
        pl.semaphore_signal(barrier, inc=1, device_id=Place.at(p // NY, p % NY, me.z, me.core), device_id_type=MESH)

    @pl.loop(1, NZ)
    def _(o):
        d = (me.z + o) % NZ
        pl.semaphore_signal(barrier, inc=1, device_id=Place.at(me.x, me.y, d, me.core), device_id_type=MESH)

    return 1 + NXY - 1 + NZ - 1

GROUP, FR, COLS, ROWN = 8, 4, 32, 16
POS = COLS * ROWN
NG = NX * NZ


class Ring:
    def __init__(self):
        f, r = lax.axis_index("frame"), lax.axis_index("row")
        self.g, self.y_lo, self.r = f // 2, f % 2, r
        self.s = (r // 2) * 4 + self.y_lo * 2 + r % 2

    @staticmethod
    def parts(s):
        return (s // 2) % 2, (s // 4) * 2 + s % 2

    @staticmethod
    def at(g, s):
        y_lo, r = Ring.parts(s)
        return (g * 2 + y_lo, r)


class Field:
    def __init__(self, ref, ring, own, step, send, recv):
        self.ref, self.ring, self.own, self.step, self.send, self.recv = ref, ring, own, step, send, recv
        self.sends = []

    def clear(self):
        far = 0 if self.own else FR
        self.ref[far : far + 2] = jnp.zeros((2, COLS + 2, ROWN, CH), BF16)
        for col in (0, COLS + 1):
            self.ref[self.own : self.own + FR, col] = jnp.zeros((FR, ROWN, CH), BF16)

    def put(self, f, value):
        self.ref[self.own + f, 1 : COLS + 1] = value.astype(BF16).reshape(COLS, ROWN, CH)

    def to_left(self):
        return self.ring.s > 0

    def to_right(self):
        return self.ring.s < GROUP - 1

    def has_target(self):
        return self.ring.g < NG - 1 if self.step > 0 else self.ring.g > 0

    def has_source(self):
        return self.ring.g > 0 if self.step > 0 else self.ring.g < NG - 1

    def copy(self, frames, col, to_frames, to_col, g, s, i):
        return remote(self.ref.at[frames, col], self.ref.at[to_frames, to_col], self.send.at[i], self.recv.at[i], Ring.at(g, s))

    def edges(self, q):
        g, s = self.ring.g, self.ring.s
        frames = pl.ds(self.own + 2 * q, 2)

        @pl.when(self.to_left())
        def _():
            self.copy(frames, 1, frames, COLS + 1, g, s - 1, 2 * q).start()

        @pl.when(self.to_right())
        def _():
            self.copy(frames, COLS, frames, 0, g, s + 1, 2 * q + 1).start()

    def await_edges(self, q):
        self._edges(q, self.recv, self.to_right(), self.to_left())

    def _edges(self, q, sem, left, right):
        view = self.ref.at[pl.ds(self.own + 2 * q, 2), 0]

        @pl.when(left)
        def _():
            pltpu.make_async_copy(view, view, sem.at[2 * q]).wait()

        @pl.when(right)
        def _():
            pltpu.make_async_copy(view, view, sem.at[2 * q + 1]).wait()

    def frames(self):
        g, s = self.ring.g + self.step, self.ring.s
        mine, theirs = (pl.ds(FR, 2), pl.ds(0, 2)) if self.step > 0 else (pl.ds(0, 2), pl.ds(FR, 2))
        body = pl.ds(1, COLS)

        @pl.when(self.has_target())
        def _():
            self.copy(mine, body, theirs, body, g, s, 4).start()

        @pl.when(self.has_target() & self.to_left())
        def _():
            self.copy(mine, 1, theirs, COLS + 1, g, s - 1, 5).start()

        @pl.when(self.has_target() & self.to_right())
        def _():
            self.copy(mine, COLS, theirs, 0, g, s + 1, 6).start()

    def _frames(self, sem, there, left, right):
        body, col = self.ref.at[pl.ds(0, 2), pl.ds(1, COLS)], self.ref.at[pl.ds(0, 2), 0]

        @pl.when(there)
        def _():
            pltpu.make_async_copy(body, body, sem.at[4]).wait()

        @pl.when(there & left)
        def _():
            pltpu.make_async_copy(col, col, sem.at[5]).wait()

        @pl.when(there & right)
        def _():
            pltpu.make_async_copy(col, col, sem.at[6]).wait()

    def await_frames(self):
        self._frames(self.recv, self.has_source(), self.to_right(), self.to_left())

    def finish(self):
        for q in range(2):
            self._edges(q, self.send, self.to_left(), self.to_right())
        self._frames(self.send, self.has_target(), self.to_left(), self.to_right())

    def slab(self, p, k, c):
        return self.ref[2 * p + k, c : c + COLS].reshape(POS, CH)


def build_weights(kernel, ahead, back, sem):
    zero = jnp.zeros((CH, CH), BF16)
    for k, j in ((0, 1), (3, 0)):
        @pl.loop(0, 9)
        def _(bc):
            b, c = bc // 3, bc % 3
            ahead[pl.ds(pl.multiple_of((c * 4 + k) * CH, CH), CH), pl.ds(pl.multiple_of((b * 2 + j) * CH, CH), CH)] = zero
            back[pl.ds(pl.multiple_of((b * 2 + j) * CH, CH), CH), pl.ds(pl.multiple_of((c * 4 + k) * CH, CH), CH)] = zero

    @pl.loop(0, 27)
    def _(tap):
        a, b, c = tap // 9, (tap // 3) % 3, tap % 3
        for j in range(2):
            k = a + j
            pltpu.make_async_copy(
                kernel.at[tap],
                ahead.at[pl.ds(pl.multiple_of((c * 4 + k) * CH, CH), CH), pl.ds(pl.multiple_of((b * 2 + j) * CH, CH), CH)],
                sem.at[0]).start()
            k = j + 2 - a
            pltpu.make_async_copy(
                kernel.at[tap],
                back.at[pl.ds(pl.multiple_of(((2 - b) * 2 + j) * CH, CH), CH), pl.ds(pl.multiple_of(((2 - c) * 4 + k) * CH, CH), CH)],
                sem.at[1]).start()


def await_weights(ahead, back, sem):
    view = ahead.at[pl.ds(0, 54 * CH * CH // ahead.shape[1])]
    pltpu.make_async_copy(view, view, sem.at[0]).wait()
    view = back.at[pl.ds(0, 54 * CH * CH // back.shape[1])]
    pltpu.make_async_copy(view, view, sem.at[1]).wait()


def row_index(width):
    return lax.broadcasted_iota(jnp.int32, (POS, width), 0) % ROWN


def from_above(value):
    return jnp.where(row_index(value.shape[1]) == 0, 0.0, pltpu.roll(value, 1, axis=0))


def from_below(value):
    return jnp.where(row_index(value.shape[1]) == ROWN - 1, 0.0, pltpu.roll(value, POS - 1, axis=0))


def convolve(field, weights, p, contract):
    lhs = jnp.concatenate([field.slab(p, k, c) for c in range(3) for k in range(4)], axis=1)
    rows = lax.dot_general(lhs, weights[...], (((1,), (contract,)), ((), ())), preferred_element_type=F32)
    above, level, below = (rows[:, b * 2 * CH : (b + 1) * 2 * CH] for b in range(3))
    return level + from_above(above) + from_below(below)


def store_turned(turned, delta, p):
    for b, value in enumerate((from_below(delta), delta, from_above(delta))):
        turned[b * 2 * CH : (b + 1) * 2 * CH, p * POS : (p + 1) * POS] = value.astype(BF16).T


def weight_grads(field, turned, part, scale):
    for c in range(3):
        rhs = jnp.concatenate(
            [jnp.concatenate([field.slab(p, k, c) for k in range(4)], axis=1) for p in range(2)], axis=0)
        sums = lax.dot_general(turned[...], rhs, (((1,), (0,)), ((), ())), preferred_element_type=F32)
        for b in range(3):
            for a in range(3):
                one = sums[2 * b * CH : (2 * b + 1) * CH, a * CH : (a + 1) * CH]
                two = sums[(2 * b + 1) * CH : (2 * b + 2) * CH, (a + 1) * CH : (a + 2) * CH]
                tap = (a * 3 + b) * 3 + c
                part[tap * CH : (tap + 1) * CH, :] = ((one + two) * scale).T.astype(BF16)


def swap(value):
    return jnp.swapaxes(value, 0, 1)


def spread(ring, source, stage, send, recv, own):
    @pl.loop(1, GROUP)
    def _(o):
        d = (ring.s + o) % GROUP
        cols = pl.ds(pl.multiple_of(d * COLS, COLS), COLS)
        remote(source.at[:, :, cols], stage.at[pl.ds(2 * ring.y_lo, 2), pl.ds(4 * ring.r, 4)], send, recv, Ring.at(ring.g, d)).start()

    cols = pl.ds(pl.multiple_of(ring.s * COLS, COLS), COLS)
    pltpu.make_async_copy(source.at[:, :, cols], stage.at[pl.ds(2 * ring.y_lo, 2), pl.ds(4 * ring.r, 4)], own).start()


def give_back(ring, stage, result, send, recv, own):
    cols = pl.ds(pl.multiple_of(ring.s * COLS, COLS), COLS)

    @pl.loop(1, GROUP)
    def _(o):
        d = (ring.s + o) % GROUP
        half, quarter = Ring.parts(d)
        remote(stage.at[pl.ds(2 * half, 2), pl.ds(4 * quarter, 4)], result.at[:, :, cols], send, recv, Ring.at(ring.g, d)).start()

    pltpu.make_async_copy(stage.at[pl.ds(2 * ring.y_lo, 2), pl.ds(4 * ring.r, 4)], result.at[:, :, cols], own).start()


def await_blocks(flat, sem, own):
    take(flat, (GROUP - 1) * 2 * 4 * COLS, sem)
    take(flat, 2 * 4 * COLS, own)


def kernel(scale, clip, cotangent, first_kernel, second_kernel, critic_map, clip_grad, full_first, full_second,
           clip_a, act_a, second_a, first_a, first_w, first_wt, second_w, second_wt, stage, cot_f, slopes, turned,
           part, other, slots, piece, tiles,
           red_send, red_recv, halo_send, halo_recv, block_send, block_recv, block_own, weight_sem):
    me, ring = Place(), Ring()
    clips = Field(clip_a, ring, 2, 1, halo_send.at[0], halo_recv.at[0])
    acts = Field(act_a, ring, 2, 1, halo_send.at[1], halo_recv.at[1])
    seconds = Field(second_a, ring, 0, -1, halo_send.at[2], halo_recv.at[2])
    firsts = Field(first_a, ring, 0, -1, halo_send.at[3], halo_recv.at[3])
    fields = (clips, acts, seconds, firsts)
    first_sum, second_sum = (
        AllReduce(me, part.at[i], full, other.at[i], slots.at[i], piece.at[i], tiles.at[i], red_send.at[i], red_recv.at[i])
        for i, full in enumerate((full_first, full_second)))

    for field in fields:
        field.clear()

    barrier = pltpu.get_barrier_semaphore()
    count = greet_reduce_peers(me, barrier)

    @pl.loop(1, GROUP)
    def _(o):
        pl.semaphore_signal(barrier, inc=1, device_id=Ring.at(ring.g, (ring.s + o) % GROUP), device_id_type=MESH)

    count = count + GROUP - 1
    for step in (-1, 1):
        for side in (-1, 0, 1):
            g, s = ring.g + step, ring.s + side
            there = (g >= 0) & (g < NG) & (s >= 0) & (s < GROUP)

            @pl.when(there)
            def _():
                pl.semaphore_signal(barrier, inc=1, device_id=Ring.at(g, s), device_id_type=MESH)

            count = count + jnp.where(there, 1, 0)
    pl.semaphore_wait(barrier, count)

    spread(ring, clip, stage.at[0], block_send.at[0], block_recv.at[0], block_own.at[0])
    spread(ring, cotangent, stage.at[1], block_send.at[1], block_recv.at[1], block_own.at[1])
    build_weights(first_kernel, first_w, first_wt, weight_sem.at[0])
    build_weights(second_kernel, second_w, second_wt, weight_sem.at[1])
    for i in range(2):
        part[i, 27 * CH :, :] = jnp.zeros((CH, CH), BF16)

    await_blocks(full_first, block_recv.at[0], block_own.at[0])
    for f in range(FR):
        clip_a[2 + f, 1 : COLS + 1] = swap(stage[0, f])
    clips.edges(0)
    clips.edges(1)
    clips.frames()
    await_weights(first_w, first_wt, weight_sem.at[0])
    await_weights(second_w, second_wt, weight_sem.at[1])
    clips.await_edges(0)
    clips.await_edges(1)

    def sigmoid_slope(z):
        sigma = jax.nn.sigmoid(z)
        return sigma, sigma * (1.0 + z * (1.0 - sigma))

    def first_layer(p):
        pre = convolve(clips, first_w, p, 0)
        sigma, slope = sigmoid_slope(pre)
        act = pre * sigma
        for j in range(2):
            acts.put(2 * p + j, act[:, j * CH : (j + 1) * CH])
        slopes[p] = slope

    def second_layer(p):
        pre = convolve(acts, second_w, p, 0)
        sigma, slope = sigmoid_slope(pre)
        critic = pre * sigma
        delta = slope * jnp.concatenate(
            [cot_f[2 * p + j].reshape(POS, CH).astype(F32) for j in range(2)], axis=1)
        for j in range(2):
            half = slice(j * CH, (j + 1) * CH)
            stage[2, 2 * p + j] = swap(critic[:, half].astype(BF16).reshape(COLS, ROWN, CH))
            seconds.put(2 * p + j, delta[:, half])
        store_turned(turned, delta, p)

    def back_layer(p):
        delta = convolve(seconds, second_wt, p, 1) * slopes[p]
        for j in range(2):
            firsts.put(2 * p + j, delta[:, j * CH : (j + 1) * CH])
        store_turned(turned, delta, p)

    def input_layer(p):
        back = convolve(firsts, first_wt, p, 1)
        for j in range(2):
            stage[0, 2 * p + j] = swap(back[:, j * CH : (j + 1) * CH].astype(BF16).reshape(COLS, ROWN, CH))

    first_layer(1)
    acts.edges(1)
    acts.frames()
    clips.await_frames()
    first_layer(0)
    acts.edges(0)
    await_blocks(full_first, block_recv.at[1], block_own.at[1])
    for f in range(FR):
        cot_f[f] = swap(stage[1, f])
    acts.await_edges(1)
    acts.await_edges(0)
    second_layer(1)
    seconds.edges(1)
    acts.await_frames()
    second_layer(0)
    seconds.frames()
    seconds.edges(0)
    give_back(ring, stage.at[2], critic_map, block_send.at[2], block_recv.at[2], block_own.at[2])
    weight_grads(acts, turned, part.at[1], scale)
    second_sum.scatter_core()
    seconds.await_edges(0)
    seconds.await_edges(1)
    back_layer(0)
    firsts.frames()
    firsts.edges(0)
    second_sum.scatter_xy()
    seconds.await_frames()
    back_layer(1)
    firsts.edges(1)
    weight_grads(clips, turned, part.at[0], scale)
    first_sum.scatter_core()
    second_sum.scatter_z()
    take(full_first, (GROUP - 1) * 2 * 4 * COLS, block_send.at[0])
    firsts.await_edges(0)
    firsts.await_edges(1)
    first_sum.scatter_xy()
    second_sum.gather_z()
    input_layer(0)
    firsts.await_frames()
    input_layer(1)
    second_sum.gather_xy()
    give_back(ring, stage.at[0], clip_grad, block_send.at[3], block_recv.at[3], block_own.at[3])
    first_sum.scatter_z()
    first_sum.gather_z()
    second_sum.gather_core()
    first_sum.gather_xy()
    first_sum.gather_core()
    second_sum.finish()
    first_sum.finish()
    for field in fields:
        field.finish()
    for i in range(1, 4):
        take(full_first, (GROUP - 1) * 2 * 4 * COLS, block_send.at[i])
    for i in range(2, 4):
        await_blocks(full_first, block_recv.at[i], block_own.at[i])


def on_device(clip, first_kernel, second_kernel, cotangent):
    cells = clip.shape[0] * lax.axis_size("frame") * clip.shape[1] * lax.axis_size("row") * clip.shape[2]
    scale = 1.0 / float(cells) ** 0.5
    vmem, anywhere = pl.BlockSpec(memory_space=pltpu.VMEM), pl.BlockSpec(memory_space=pl.ANY)
    total = jax.ShapeDtypeStruct((ROWS, CH), BF16)
    field = pltpu.VMEM((FR + 2, COLS + 2, ROWN, CH), BF16)
    dma = pltpu.SemaphoreType.DMA
    critic_map, clip_grad, first, second = pl.pallas_call(
        functools.partial(kernel, scale),
        out_shape=(jax.ShapeDtypeStruct(clip.shape, BF16), jax.ShapeDtypeStruct(clip.shape, BF16), total, total),
        in_specs=[vmem, vmem, anywhere, anywhere],
        out_specs=(vmem, vmem, vmem, vmem),
        scratch_shapes=[
            field, field, field, field,
            pltpu.VMEM((12 * CH, 6 * CH), BF16), pltpu.VMEM((6 * CH, 12 * CH), BF16),
            pltpu.VMEM((12 * CH, 6 * CH), BF16), pltpu.VMEM((6 * CH, 12 * CH), BF16),
            pltpu.VMEM((3, FR, ROWN, COLS, CH), BF16),
            pltpu.VMEM((FR, COLS, ROWN, CH), BF16),
            pltpu.VMEM((2, POS, 2 * CH), F32),
            pltpu.VMEM((6 * CH, 2 * POS), BF16),
            pltpu.VMEM((2, ROWS, CH), BF16),
            pltpu.VMEM((2, HALF, CH), BF16),
            pltpu.VMEM((2, NXY * BLK, CH), BF16),
            pltpu.VMEM((2, BLK, CH), BF16),
            pltpu.VMEM((2, NZ * TILE, CH), BF16),
            dma((2, 6)), dma((2, 6)), dma((4, 7)), dma((4, 7)), dma((4,)), dma((4,)), dma((4,)), dma((2, 2)),
        ],
        compiler_params=pltpu.CompilerParams(collective_id=0, has_side_effects=True, vmem_limit_bytes=60 << 20),
    )(clip, cotangent, first_kernel.reshape(27, CH, CH), second_kernel.reshape(27, CH, CH))

    def whole(total):
        return total[: 27 * CH].reshape(3, 3, 3, CH, CH).astype(F32)

    return critic_map, clip_grad, whole(first), whole(second)


def solution(mesh):
    placed = (P("frame", "row", None, None), P(), P(), P("frame", "row", None, None))
    return jax.shard_map(
        on_device,
        mesh=mesh,
        in_specs=placed,
        out_specs=(P("frame", "row", None, None), P("frame", "row", None, None), P(), P()),
        check_vma=False,
    )
```

profile of v0, /device:TPU:1, one launch (start us, length us, event | category | flops | bytes accessed | tf_op | source)
XLA Modules:
  0.0 94.8 jit_solution(6128995872228810779)
XLA Ops:
  0.6 88.4 %shard_map.75 = (bf16[2,4,256,128]{3,2,1,0:T(8,128)(2,1)}, bf16[2,4,256,128]{3,2,1,0:T(8,128)(2,1)}, bf16[3584,128]{1,0:T(8,128)(2,1)}, bf16[3584,128]{1,0:T(8,128)(2,1)}) custom-call(bf16[2,4,256,128]{3,2,1,0:T(8,128)(2,1)} %clip.1, bf16[2,4,256,128]{3,2,1,0:T(8,128)(2,1)} %cotangent.1, bf16[27,128,128]{2,1,0:T(8,128)(2,1)} %bitcast.8, ...), custom_call_target="tpu_custom_call" | custom-call | tf_op jit(solution)/shard_map/pallas_call | solution.py:557
  89.0 1.2 %slice.6 = bf16[3456,128]{1,0:T(8,128)(2,1)S(1)} slice(bf16[3584,128]{1,0:T(8,128)(2,1)} %get-tuple-element.10), slice={[0:3456], [0:128]} | slice | bytes 1769472 | tf_op jit(solution)/shard_map/slice | solution.py:581
  90.3 0.0 copy-start
  90.3 1.4 %convert.2 = f32[3,3,3,128,128]{4,3,2,1,0:T(8,128)} convert(bf16[3,3,3,128,128]{4,3,2,1,0:T(8,128)(2,1)S(1)} %bitcast.6) | non-fusion elementwise | flops 442368 | bytes 2654208 | tf_op jit(solution)/shard_map/convert_element_type | solution.py:581
  91.7 0.0 copy-done
  91.7 0.1 slice.7
  91.8 0.0 copy-start.2
  91.8 0.0 copy-start.1
  91.8 1.4 %convert.3 = f32[3,3,3,128,128]{4,3,2,1,0:T(8,128)} convert(bf16[3,3,3,128,128]{4,3,2,1,0:T(8,128)(2,1)S(1)} %bitcast.7) | non-fusion elementwise | flops 442368 | bytes 2654208 | tf_op jit(solution)/shard_map/convert_element_type | solution.py:581
  93.2 0.0 copy-done.2
  93.2 0.8 copy.10
  94.0 0.0 copy-done.1
  94.0 0.8 copy.11
Async XLA Ops:
  90.3 1.4 %copy-start = (bf16[3584,128]{1,0:T(8,128)(2,1)S(1)}, bf16[3584,128]{1,0:T(8,128)(2,1)}, u32[]{:S(2)}) copy-start(bf16[3584,128]{1,0:T(8,128)(2,1)} %get-tuple-element.11) | copy-start | bytes 2752516
  91.8 1.4 %copy-start.2 = (bf16[2,4,256,128]{3,2,1,0:T(8,128)(2,1)S(1)}, bf16[2,4,256,128]{3,2,1,0:T(8,128)(2,1)}, u32[]{:S(2)}) copy-start(bf16[2,4,256,128]{3,2,1,0:T(8,128)(2,1)} %get-tuple-element.16) | copy-start | bytes 1572868
  91.8 2.2 %copy-start.1 = (bf16[2,4,256,128]{3,2,1,0:T(8,128)(2,1)S(1)}, bf16[2,4,256,128]{3,2,1,0:T(8,128)(2,1)}, u32[]{:S(2)}) copy-start(bf16[2,4,256,128]{3,2,1,0:T(8,128)(2,1)} %get-tuple-element.17) | copy-start | bytes 1572868
where the time goes:
time: 94.9 us; the launch traced here: 94.8 us
  Pallas kernels  88.4 us (93%)
  local copies, waits for them, and re-layouts  2.88 us (3%)
  other arithmetic  2.81 us (3%)
    pallas_call x1, Pallas kernels, on_device(): pl.pallas_call(functools.partial(kernel, scale), out_shape=(jax.ShapeDtyp...  88.4 us
    convert_element_type x2, other arithmetic, whole(): return total[:27 * CH].reshape(3, 3, 3, CH, CH).astype(F32)  2.81 us

commit v1 on v0

v1 whole, which is shorter than its diff:
```python
import functools

import jax
import jax.numpy as jnp
from jax import lax
from jax.experimental import pallas as pl
from jax.experimental.pallas import tpu as pltpu
from jax.sharding import PartitionSpec as P

MESH = pl.DeviceIdType.MESH
BF16, F32 = jnp.bfloat16, jnp.float32
CH = 128

NX, NY, NZ = 4, 4, 8
NXY = NX * NY
BLK = 112
HALF = NXY * BLK
ROWS = 2 * HALF
TILE = 16
ZT = BLK // TILE


class Place:
    def __init__(self):
        f, r = lax.axis_index("frame"), lax.axis_index("row")
        self.x, self.z = f // (2 * NZ), (f // 2) % NZ
        self.y, self.core = (r // 2) * 2 + f % 2, r % 2
        self.p = self.x * NY + self.y

    @staticmethod
    def at(x, y, z, core):
        return ((x * NZ + z) * 2 + y % 2, (y // 2) * 2 + core)


def remote(src, dst, send, recv, device):
    return pltpu.make_async_remote_copy(
        src_ref=src, dst_ref=dst, send_sem=send, recv_sem=recv, device_id=device, device_id_type=MESH)


def take(ref, rows, sem):
    view = ref.at[pl.ds(0, rows)]
    pltpu.make_async_copy(view, view, sem).wait()


def rows_of(start, size):
    return pl.ds(pl.multiple_of(start, TILE), size)


class AllReduce:
    A, B = (256, 64), (192, 48)
    START_B = NX * 256

    def __init__(self, me, part, full, other, slots, near, piece, tiles, send, recv):
        self.me, self.part, self.full = me, part, full
        self.other, self.slots, self.near, self.piece, self.tiles = other, slots, near, piece, tiles
        self.send, self.recv = send, recv
        self.base = me.core * HALF

    def x_peer(self, o):
        x = (self.me.x + o) % NX
        return x, Place.at(x, self.me.y, self.me.z, self.me.core)

    def y_peer(self, o):
        y = (self.me.y + o) % NY
        return y, Place.at(self.me.x, y, self.me.z, self.me.core)

    def z_peer(self, o):
        d = (self.me.z + o) % NZ
        return d, Place.at(self.me.x, self.me.y, d, self.me.core)

    def twin(self):
        return Place.at(self.me.x, self.me.y, self.me.z, 1 - self.me.core)

    def row_a(self, x, y):
        return self.base + x * self.A[0] + y * self.A[1]

    def row_b(self, x, y):
        return self.base + self.START_B + y * self.B[0] + x * self.B[1]

    def push(self, stage, source, start, target, to, size, peer):
        remote(source.at[rows_of(start, size)], target.at[rows_of(to, size)], self.send.at[stage], self.recv.at[stage], peer).start()

    def scatter_core(self):
        self.push(0, self.part, (1 - self.me.core) * HALF, self.other, 0, HALF, self.twin())

    def scatter_far(self):
        me = self.me
        take(self.other, HALF, self.recv.at[0])

        @pl.loop(0, HALF // 128)
        def _(i):
            mine = rows_of(self.base + i * 128, 128)
            total = self.part[mine, :].astype(F32) + self.other[rows_of(i * 128, 128), :].astype(F32)
            self.part[mine, :] = total.astype(BF16)

        @pl.loop(1, NX)
        def _(o):
            x, peer = self.x_peer(o)
            self.push(1, self.part, self.row_a(x, 0), self.slots, me.x * self.A[0], self.A[0], peer)
            y, peer = self.y_peer(o)
            self.push(1, self.part, self.row_b(0, y), self.slots, self.START_B + me.y * self.B[0], self.B[0], peer)

    def scatter_near(self):
        me = self.me
        take(self.slots, 3 * (self.A[0] + self.B[0]), self.recv.at[1])

        @pl.loop(0, 4)
        def _(i):
            for start, slot, mine, pitch, size in (
                (self.row_a(me.x, 0), 0, me.x, self.A[0], self.A[1]),
                (self.row_b(0, me.y), self.START_B, me.y, self.B[0], self.B[1])):
                rows = rows_of(start + i * size, size)
                total = self.part[rows, :].astype(F32)
                for o in range(1, 4):
                    total = total + self.slots[rows_of(slot + ((mine + o) % 4) * pitch + i * size, size), :].astype(F32)
                self.part[rows, :] = total.astype(BF16)

        @pl.loop(1, NX)
        def _(o):
            y, peer = self.y_peer(o)
            self.push(2, self.part, self.row_a(me.x, y), self.near, me.y * self.A[1], self.A[1], peer)
            x, peer = self.x_peer(o)
            self.push(2, self.part, self.row_b(x, me.y), self.near, NY * self.A[1] + me.x * self.B[1], self.B[1], peer)

    def scatter_z(self):
        me = self.me
        take(self.near, 3 * (self.A[1] + self.B[1]), self.recv.at[2])
        for start, slot, mine, size, to in (
            (self.row_a(me.x, me.y), 0, me.y, self.A[1], 0),
            (self.row_b(me.x, me.y), NY * self.A[1], me.x, self.B[1], self.A[1])):
            total = self.part[rows_of(start, size), :].astype(F32)
            for o in range(1, 4):
                total = total + self.near[rows_of(slot + ((mine + o) % 4) * size, size), :].astype(F32)
            self.piece[to : to + size, :] = total.astype(BF16)

        @pl.loop(1, NZ)
        def _(o):
            d, peer = self.z_peer(o)

            @pl.when(d < ZT)
            def _():
                self.push(3, self.piece, d * TILE, self.tiles, me.z * TILE, TILE, peer)

    def gather_z(self):
        me = self.me

        @pl.when(me.z < ZT)
        def _():
            take(self.tiles, (NZ - 1) * TILE, self.recv.at[3])
            total = self.piece[rows_of(me.z * TILE, TILE), :].astype(F32)
            for o in range(1, NZ):
                d = (me.z + o) % NZ
                total = total + self.tiles[rows_of(d * TILE, TILE), :].astype(F32)
            in_a = self.A[1] // TILE
            row = jnp.where(me.z < in_a, self.row_a(me.x, me.y) + me.z * TILE, self.row_b(me.x, me.y) + (me.z - in_a) * TILE)
            self.full[rows_of(row, TILE), :] = total.astype(BF16)

            @pl.loop(1, NZ)
            def _(o):
                d, peer = self.z_peer(o)
                self.push(4, self.full, row, self.full, row, TILE, peer)

    def gather_near(self):
        me = self.me

        @pl.when(me.z < ZT)
        def _():
            take(self.full, (ZT - 1) * TILE, self.recv.at[4])

        @pl.when(me.z >= ZT)
        def _():
            take(self.full, ZT * TILE, self.recv.at[4])

        a, b = self.row_a(me.x, me.y), self.row_b(me.x, me.y)

        @pl.loop(1, NX)
        def _(o):
            self.push(5, self.full, a, self.full, a, self.A[1], self.y_peer(o)[1])
            self.push(5, self.full, b, self.full, b, self.B[1], self.x_peer(o)[1])

    def gather_far(self):
        me = self.me
        take(self.full, 3 * (self.A[1] + self.B[1]), self.recv.at[5])
        a, b = self.row_a(me.x, 0), self.row_b(0, me.y)

        @pl.loop(1, NX)
        def _(o):
            self.push(6, self.full, a, self.full, a, self.A[0], self.x_peer(o)[1])
            self.push(6, self.full, b, self.full, b, self.B[0], self.y_peer(o)[1])

    def gather_core(self):
        take(self.full, 3 * (self.A[0] + self.B[0]), self.recv.at[6])
        self.push(7, self.full, self.base, self.full, self.base, HALF, self.twin())

    def finish(self):
        me = self.me
        take(self.full, HALF, self.recv.at[7])
        take(self.part, HALF, self.send.at[0])
        take(self.part, 3 * (self.A[0] + self.B[0]), self.send.at[1])
        take(self.part, 3 * (self.A[1] + self.B[1]), self.send.at[2])

        @pl.when(me.z < ZT)
        def _():
            take(self.piece, (ZT - 1) * TILE, self.send.at[3])
            take(self.full, (NZ - 1) * TILE, self.send.at[4])

        @pl.when(me.z >= ZT)
        def _():
            take(self.piece, ZT * TILE, self.send.at[3])

        take(self.full, 3 * (self.A[1] + self.B[1]), self.send.at[5])
        take(self.full, 3 * (self.A[0] + self.B[0]), self.send.at[6])
        take(self.full, HALF, self.send.at[7])


def greet_reduce_peers(me, barrier):
    pl.semaphore_signal(barrier, inc=1, device_id=Place.at(me.x, me.y, me.z, 1 - me.core), device_id_type=MESH)

    @pl.loop(1, NXY)
    def _(o):
        p = (me.p + o) % NXY
        pl.semaphore_signal(barrier, inc=1, device_id=Place.at(p // NY, p % NY, me.z, me.core), device_id_type=MESH)

    @pl.loop(1, NZ)
    def _(o):
        d = (me.z + o) % NZ
        pl.semaphore_signal(barrier, inc=1, device_id=Place.at(me.x, me.y, d, me.core), device_id_type=MESH)

    return 1 + NXY - 1 + NZ - 1

GROUP, FR, COLS, ROWN = 8, 4, 32, 16
POS = COLS * ROWN
NG = NX * NZ


class Ring:
    def __init__(self):
        f, r = lax.axis_index("frame"), lax.axis_index("row")
        self.g, self.y_lo, self.r = f // 2, f % 2, r
        self.s = (r // 2) * 4 + self.y_lo * 2 + r % 2

    @staticmethod
    def parts(s):
        return (s // 2) % 2, (s // 4) * 2 + s % 2

    @staticmethod
    def at(g, s):
        y_lo, r = Ring.parts(s)
        return (g * 2 + y_lo, r)


class Field:
    def __init__(self, ref, ring, own, halo, step, whole, send, recv):
        self.ref, self.ring, self.own, self.halo, self.step, self.whole = ref, ring, own, halo, step, whole
        self.send, self.recv = send, recv
        self.width = COLS + 2 * halo

    def clear(self):
        far = 0 if self.own else FR
        self.ref[far : far + 2] = jnp.zeros((2, self.width, ROWN, CH), BF16)
        for col in (0, COLS + self.halo):
            self.ref[self.own : self.own + FR, col : col + self.halo] = jnp.zeros((FR, self.halo, ROWN, CH), BF16)

    def put(self, f, value):
        self.ref[self.own + f, self.halo : self.halo + COLS] = value.astype(BF16).reshape(COLS, ROWN, CH)

    def to_left(self):
        return self.ring.s > 0

    def to_right(self):
        return self.ring.s < GROUP - 1

    def has_target(self):
        return self.ring.g < NG - 1 if self.step > 0 else self.ring.g > 0

    def has_source(self):
        return self.ring.g > 0 if self.step > 0 else self.ring.g < NG - 1

    def copy(self, frames, col, to_frames, to_col, width, g, s, i):
        return remote(self.ref.at[frames, pl.ds(col, width)], self.ref.at[to_frames, pl.ds(to_col, width)],
                      self.send.at[i], self.recv.at[i], Ring.at(g, s))

    def edge(self, frames, to_frames, side, g, i):
        halo, s = self.halo, self.ring.s
        source, target = (halo, COLS + halo) if side < 0 else (COLS, 0)
        self.copy(frames, source, to_frames, target, halo, g, s + side, i).start()

    def edges(self, q):
        frames = pl.ds(self.own + 2 * q, 2)

        @pl.when(self.to_left())
        def _():
            self.edge(frames, frames, -1, self.ring.g, 2 * q)

        @pl.when(self.to_right())
        def _():
            self.edge(frames, frames, 1, self.ring.g, 2 * q + 1)

    def await_edges(self, q):
        self._edges(q, self.recv, self.to_right(), self.to_left())

    def _edges(self, q, sem, left, right):
        view = self.ref.at[pl.ds(self.own + 2 * q, 2), pl.ds(0, self.halo)]

        @pl.when(left)
        def _():
            pltpu.make_async_copy(view, view, sem.at[2 * q]).wait()

        @pl.when(right)
        def _():
            pltpu.make_async_copy(view, view, sem.at[2 * q + 1]).wait()

    def span(self):
        return (0, self.width) if self.whole else (self.halo, COLS)

    def frames(self):
        g, s = self.ring.g + self.step, self.ring.s
        mine, theirs = (pl.ds(FR, 2), pl.ds(0, 2)) if self.step > 0 else (pl.ds(0, 2), pl.ds(FR, 2))
        start, width = self.span()

        @pl.when(self.has_target())
        def _():
            self.copy(mine, start, theirs, start, width, g, s, 4).start()

        if self.whole:
            return

        @pl.when(self.has_target() & self.to_left())
        def _():
            self.edge(mine, theirs, -1, g, 5)

        @pl.when(self.has_target() & self.to_right())
        def _():
            self.edge(mine, theirs, 1, g, 6)

    def _frames(self, sem, there, left, right):
        start, width = self.span()
        body, col = self.ref.at[pl.ds(0, 2), pl.ds(start, width)], self.ref.at[pl.ds(0, 2), pl.ds(0, self.halo)]

        @pl.when(there)
        def _():
            pltpu.make_async_copy(body, body, sem.at[4]).wait()

        if self.whole:
            return

        @pl.when(there & left)
        def _():
            pltpu.make_async_copy(col, col, sem.at[5]).wait()

        @pl.when(there & right)
        def _():
            pltpu.make_async_copy(col, col, sem.at[6]).wait()

    def await_frames(self):
        self._frames(self.recv, self.has_source(), self.to_right(), self.to_left())

    def finish(self):
        if not self.whole:
            for q in range(2):
                self._edges(q, self.send, self.to_left(), self.to_right())
        self._frames(self.send, self.has_target(), self.to_left(), self.to_right())

    def slab(self, p, k, start, width):
        return self.ref[2 * p + k, start : start + width].reshape(width * ROWN, CH)


def build_weights(kernel, ahead, back, sem):
    zero = jnp.zeros((CH, CH), BF16)
    for k, j in ((0, 1), (3, 0)):
        @pl.loop(0, 9)
        def _(bc):
            b, c = bc // 3, bc % 3
            ahead[pl.ds(pl.multiple_of((c * 4 + k) * CH, CH), CH), pl.ds(pl.multiple_of((b * 2 + j) * CH, CH), CH)] = zero
            back[pl.ds(pl.multiple_of((b * 2 + j) * CH, CH), CH), pl.ds(pl.multiple_of((c * 4 + k) * CH, CH), CH)] = zero

    @pl.loop(0, 27)
    def _(tap):
        a, b, c = tap // 9, (tap // 3) % 3, tap % 3
        for j in range(2):
            k = a + j
            pltpu.make_async_copy(
                kernel.at[tap],
                ahead.at[pl.ds(pl.multiple_of((c * 4 + k) * CH, CH), CH), pl.ds(pl.multiple_of((b * 2 + j) * CH, CH), CH)],
                sem.at[0]).start()
            k = j + 2 - a
            pltpu.make_async_copy(
                kernel.at[tap],
                back.at[pl.ds(pl.multiple_of(((2 - b) * 2 + j) * CH, CH), CH), pl.ds(pl.multiple_of(((2 - c) * 4 + k) * CH, CH), CH)],
                sem.at[1]).start()


def await_weights(ahead, back, sem):
    view = ahead.at[pl.ds(0, 54 * CH * CH // ahead.shape[1])]
    pltpu.make_async_copy(view, view, sem.at[0]).wait()
    view = back.at[pl.ds(0, 54 * CH * CH // back.shape[1])]
    pltpu.make_async_copy(view, view, sem.at[1]).wait()


def row_index(shape):
    return lax.broadcasted_iota(jnp.int32, shape, 0) % ROWN


def from_above(value):
    return jnp.where(row_index(value.shape) == 0, 0.0, pltpu.roll(value, 1, axis=0))


def from_below(value):
    return jnp.where(row_index(value.shape) == ROWN - 1, 0.0, pltpu.roll(value, value.shape[0] - 1, axis=0))


def convolve(field, weights, p, contract):
    width = field.width - 2
    lhs = jnp.concatenate([field.slab(p, k, c, width) for c in range(3) for k in range(4)], axis=1)
    rows = lax.dot_general(lhs, weights[...], (((1,), (contract,)), ((), ())), preferred_element_type=F32)
    above, level, below = (rows[:, b * 2 * CH : (b + 1) * 2 * CH] for b in range(3))
    return level + from_above(above) + from_below(below)


def store_turned(turned, delta, p):
    for b, value in enumerate((from_below(delta), delta, from_above(delta))):
        turned[b * 2 * CH : (b + 1) * 2 * CH, p * POS : (p + 1) * POS] = value.astype(BF16).T


def weight_grads(field, turned, part, scale):
    for c in range(3):
        rhs = jnp.concatenate(
            [jnp.concatenate([field.slab(p, k, field.halo - 1 + c, COLS) for k in range(4)], axis=1) for p in range(2)], axis=0)
        sums = lax.dot_general(turned[...], rhs, (((1,), (0,)), ((), ())), preferred_element_type=F32)
        for b in range(3):
            for a in range(3):
                one = sums[2 * b * CH : (2 * b + 1) * CH, a * CH : (a + 1) * CH]
                two = sums[(2 * b + 1) * CH : (2 * b + 2) * CH, (a + 1) * CH : (a + 2) * CH]
                tap = (a * 3 + b) * 3 + c
                part[tap * CH : (tap + 1) * CH, :] = ((one + two) * scale).T.astype(BF16)


def swap(value):
    return jnp.swapaxes(value, 0, 1)


def spread(ring, source, stage, send, recv, own):
    @pl.loop(1, GROUP)
    def _(o):
        d = (ring.s + o) % GROUP
        cols = pl.ds(pl.multiple_of(d * COLS, COLS), COLS)
        remote(source.at[:, :, cols], stage.at[pl.ds(2 * ring.y_lo, 2), pl.ds(4 * ring.r, 4)], send, recv, Ring.at(ring.g, d)).start()

    cols = pl.ds(pl.multiple_of(ring.s * COLS, COLS), COLS)
    pltpu.make_async_copy(source.at[:, :, cols], stage.at[pl.ds(2 * ring.y_lo, 2), pl.ds(4 * ring.r, 4)], own).start()


def give_back(ring, stage, result, send, recv, own):
    cols = pl.ds(pl.multiple_of(ring.s * COLS, COLS), COLS)

    @pl.loop(1, GROUP)
    def _(o):
        d = (ring.s + o) % GROUP
        half, quarter = Ring.parts(d)
        remote(stage.at[pl.ds(2 * half, 2), pl.ds(4 * quarter, 4)], result.at[:, :, cols], send, recv, Ring.at(ring.g, d)).start()

    pltpu.make_async_copy(stage.at[pl.ds(2 * ring.y_lo, 2), pl.ds(4 * ring.r, 4)], result.at[:, :, cols], own).start()


def await_blocks(flat, sem, own):
    take(flat, (GROUP - 1) * 2 * 4 * COLS, sem)
    take(flat, 2 * 4 * COLS, own)


def kernel(scale, clip_in, cotangent_in, first_kernel, second_kernel, critic_map, clip_grad, full_first, full_second,
           clip_a, act_a, second_a, first_a, first_w, first_wt, second_w, second_wt, clip, cotangent, stage, cot_f, slopes,
           turned, part, other, slots, near, piece, tiles,
           red_send, red_recv, halo_send, halo_recv, block_send, block_recv, block_own, weight_sem, load_sem):
    loads = [pltpu.make_async_copy(source, target, load_sem.at[i])
             for i, (source, target) in enumerate(((clip_in, clip), (cotangent_in, cotangent)))]
    for load in loads:
        load.start()
    me, ring = Place(), Ring()
    clips = Field(clip_a, ring, 2, 2, 1, False, halo_send.at[0], halo_recv.at[0])
    acts = Field(act_a, ring, 2, 1, 1, True, halo_send.at[1], halo_recv.at[1])
    seconds = Field(second_a, ring, 0, 1, -1, False, halo_send.at[2], halo_recv.at[2])
    firsts = Field(first_a, ring, 0, 1, -1, False, halo_send.at[3], halo_recv.at[3])
    fields = (clips, acts, seconds, firsts)
    first_sum, second_sum = (
        AllReduce(me, part.at[i], full, other.at[i], slots.at[i], near.at[i], piece.at[i], tiles.at[i],
                  red_send.at[i], red_recv.at[i])
        for i, full in enumerate((full_first, full_second)))

    for field in fields:
        field.clear()

    barrier = pltpu.get_barrier_semaphore()
    count = greet_reduce_peers(me, barrier)

    @pl.loop(1, GROUP)
    def _(o):
        pl.semaphore_signal(barrier, inc=1, device_id=Ring.at(ring.g, (ring.s + o) % GROUP), device_id_type=MESH)

    count = count + GROUP - 1
    for step in (-1, 1):
        for side in (-1, 0, 1):
            g, s = ring.g + step, ring.s + side
            there = (g >= 0) & (g < NG) & (s >= 0) & (s < GROUP)

            @pl.when(there)
            def _():
                pl.semaphore_signal(barrier, inc=1, device_id=Ring.at(g, s), device_id_type=MESH)

            count = count + jnp.where(there, 1, 0)
    build_weights(first_kernel, first_w, first_wt, weight_sem.at[0])
    for i in range(2):
        part[i, 27 * CH :, :] = jnp.zeros((CH, CH), BF16)
    loads[0].wait()
    pl.semaphore_wait(barrier, count)

    spread(ring, clip, stage.at[0], block_send.at[0], block_recv.at[0], block_own.at[0])
    loads[1].wait()
    spread(ring, cotangent, stage.at[1], block_send.at[1], block_recv.at[1], block_own.at[1])
    build_weights(second_kernel, second_w, second_wt, weight_sem.at[1])

    await_blocks(full_first, block_recv.at[0], block_own.at[0])
    for f in range(FR):
        clip_a[2 + f, 2 : COLS + 2] = swap(stage[0, f])
    clips.edges(0)
    clips.edges(1)
    clips.frames()
    await_weights(first_w, first_wt, weight_sem.at[0])
    await_weights(second_w, second_wt, weight_sem.at[1])
    clips.await_edges(0)
    clips.await_edges(1)

    def sigmoid_slope(z):
        sigma = jax.nn.sigmoid(z)
        return sigma, sigma * (1.0 + z * (1.0 - sigma))

    def first_layer(p):
        pre = convolve(clips, first_w, p, 0)
        sigma, slope = sigmoid_slope(pre)
        act = (pre * sigma).astype(BF16)
        for j in range(2):
            act_a[2 + 2 * p + j] = act[:, j * CH : (j + 1) * CH].reshape(COLS + 2, ROWN, CH)
        slopes[p] = slope[ROWN : ROWN + POS]
        pair, edge = pl.ds(2 + 2 * p, 2), jnp.zeros((2, ROWN, CH), BF16)

        @pl.when(ring.s == 0)
        def _():
            act_a[pair, 0] = edge

        @pl.when(ring.s == GROUP - 1)
        def _():
            act_a[pair, COLS + 1] = edge

    def second_layer(p):
        pre = convolve(acts, second_w, p, 0)
        sigma, slope = sigmoid_slope(pre)
        critic = pre * sigma
        delta = slope * jnp.concatenate(
            [cot_f[2 * p + j].reshape(POS, CH).astype(F32) for j in range(2)], axis=1)
        for j in range(2):
            half = slice(j * CH, (j + 1) * CH)
            stage[2, 2 * p + j] = swap(critic[:, half].astype(BF16).reshape(COLS, ROWN, CH))
            seconds.put(2 * p + j, delta[:, half])
        store_turned(turned, delta, p)

    def back_layer(p):
        delta = convolve(seconds, second_wt, p, 1) * slopes[p]
        for j in range(2):
            firsts.put(2 * p + j, delta[:, j * CH : (j + 1) * CH])
        store_turned(turned, delta, p)

    def input_layer(p):
        back = convolve(firsts, first_wt, p, 1)
        for j in range(2):
            stage[0, 2 * p + j] = swap(back[:, j * CH : (j + 1) * CH].astype(BF16).reshape(COLS, ROWN, CH))

    first_layer(1)
    acts.frames()
    clips.await_frames()
    first_layer(0)
    await_blocks(full_first, block_recv.at[1], block_own.at[1])
    for f in range(FR):
        cot_f[f] = swap(stage[1, f])
    second_layer(1)
    seconds.edges(1)
    acts.await_frames()
    second_layer(0)
    seconds.frames()
    seconds.edges(0)
    give_back(ring, stage.at[2], critic_map, block_send.at[2], block_recv.at[2], block_own.at[2])
    weight_grads(acts, turned, part.at[1], scale)
    second_sum.scatter_core()
    seconds.await_edges(0)
    seconds.await_edges(1)
    back_layer(0)
    firsts.frames()
    firsts.edges(0)
    second_sum.scatter_far()
    seconds.await_frames()
    back_layer(1)
    firsts.edges(1)
    second_sum.scatter_near()
    weight_grads(clips, turned, part.at[0], scale)
    first_sum.scatter_core()
    second_sum.scatter_z()
    take(full_first, (GROUP - 1) * 2 * 4 * COLS, block_send.at[0])
    firsts.await_edges(0)
    firsts.await_edges(1)
    first_sum.scatter_far()
    input_layer(0)
    firsts.await_frames()
    input_layer(1)
    second_sum.gather_z()
    first_sum.scatter_near()
    give_back(ring, stage.at[0], clip_grad, block_send.at[3], block_recv.at[3], block_own.at[3])
    second_sum.gather_near()
    first_sum.scatter_z()
    second_sum.gather_far()
    first_sum.gather_z()
    first_sum.gather_near()
    first_sum.gather_far()
    second_sum.gather_core()
    first_sum.gather_core()
    second_sum.finish()
    for field in fields:
        field.finish()
    for i in range(1, 4):
        take(full_first, (GROUP - 1) * 2 * 4 * COLS, block_send.at[i])
    for i in range(2, 4):
        await_blocks(full_first, block_recv.at[i], block_own.at[i])
    first_sum.finish()


def write_out(critic_in, grad_in, first_in, second_in, critic, grad, first, second):
    critic[...] = critic_in[...]
    grad[...] = grad_in[...]
    first[...] = first_in[...].astype(F32)
    second[...] = second_in[...].astype(F32)


def on_device(clip, first_kernel, second_kernel, cotangent):
    cells = clip.shape[0] * lax.axis_size("frame") * clip.shape[1] * lax.axis_size("row") * clip.shape[2]
    scale = 1.0 / float(cells) ** 0.5
    vmem, anywhere = pl.BlockSpec(memory_space=pltpu.VMEM), pl.BlockSpec(memory_space=pl.ANY)
    total = jax.ShapeDtypeStruct((ROWS, CH), BF16)
    dma = pltpu.SemaphoreType.DMA
    flat = (2 * 4 * GROUP * COLS, CH)

    def field(halo):
        return pltpu.VMEM((FR + 2, COLS + 2 * halo, ROWN, CH), BF16)

    results = pl.pallas_call(
        functools.partial(kernel, scale),
        out_shape=(jax.ShapeDtypeStruct(clip.shape, BF16), jax.ShapeDtypeStruct(clip.shape, BF16), total, total),
        in_specs=[anywhere] * 4,
        out_specs=(vmem, vmem, vmem, vmem),
        scratch_shapes=[
            field(2), field(1), field(1), field(1),
            pltpu.VMEM((12 * CH, 6 * CH), BF16), pltpu.VMEM((6 * CH, 12 * CH), BF16),
            pltpu.VMEM((12 * CH, 6 * CH), BF16), pltpu.VMEM((6 * CH, 12 * CH), BF16),
            pltpu.VMEM(clip.shape, BF16), pltpu.VMEM(clip.shape, BF16),
            pltpu.VMEM((3, FR, ROWN, COLS, CH), BF16),
            pltpu.VMEM((FR, COLS, ROWN, CH), BF16),
            pltpu.VMEM((2, POS, 2 * CH), F32),
            pltpu.VMEM((6 * CH, 2 * POS), BF16),
            pltpu.VMEM((2, ROWS, CH), BF16),
            pltpu.VMEM((2, HALF, CH), BF16),
            pltpu.VMEM((2, HALF, CH), BF16),
            pltpu.VMEM((2, HALF // 4, CH), BF16),
            pltpu.VMEM((2, BLK, CH), BF16),
            pltpu.VMEM((2, NZ * TILE, CH), BF16),
            dma((2, 8)), dma((2, 8)), dma((4, 7)), dma((4, 7)), dma((4,)), dma((4,)), dma((4,)), dma((2, 2)), dma((2,)),
        ],
        compiler_params=pltpu.CompilerParams(collective_id=0, has_side_effects=True, vmem_limit_bytes=60 << 20),
    )(clip, cotangent, first_kernel.reshape(27, CH, CH), second_kernel.reshape(27, CH, CH))
    critic_map, clip_grad, first, second = results

    steps = 4
    maps, grads = (pl.BlockSpec((rows // steps, CH), lambda i: (i, 0)) for rows in (flat[0], 27 * CH))
    whole = jax.ShapeDtypeStruct((27 * CH, CH), F32)
    critic_map, clip_grad, first, second = pl.pallas_call(
        write_out,
        grid=(steps,),
        out_shape=(jax.ShapeDtypeStruct(flat, BF16), jax.ShapeDtypeStruct(flat, BF16), whole, whole),
        in_specs=[maps, maps, grads, grads],
        out_specs=(maps, maps, grads, grads),
    )(critic_map.reshape(flat), clip_grad.reshape(flat), first, second)
    taps = (3, 3, 3, CH, CH)
    return critic_map.reshape(clip.shape), clip_grad.reshape(clip.shape), first.reshape(taps), second.reshape(taps)


def solution(mesh):
    placed = (P("frame", "row", None, None), P(), P(), P("frame", "row", None, None))
    return jax.shard_map(
        on_device,
        mesh=mesh,
        in_specs=placed,
        out_specs=(P("frame", "row", None, None), P("frame", "row", None, None), P(), P()),
        check_vma=False,
    )
```

time: 94.9 us -> 96.2 us (1.014)
  Pallas kernels: 88.4 us -> 95.4 us
  local copies, waits for them, and re-layouts: 2.88 us -> 0 us
  other arithmetic: 2.81 us -> 0 us
    pallas_call x0 -> x1, Pallas kernels: none -> 4.46 us  [on_device(): pl.pallas_call(write_out, grid=(steps,), out_shape=(jax.ShapeDtypeStruct(...]
    convert_element_type x2 -> x0, other arithmetic: 2.81 us -> none  [whole(): return total[:27 * CH].reshape(3, 3, 3, CH, CH).astype(F32)]
    pallas_call x1, Pallas kernels: 88.4 us -> 91 us  [on_device(): pl.pallas_call(functools.partial(kernel, scale), out_shape=(jax.ShapeDtyp...]
    unnamed x8 -> x0, local copies, waits for them, and re-layouts: 1.6 us -> none
    slice x2 -> x0, local copies, waits for them, and re-layouts: 1.28 us -> none  [whole(): return total[:27 * CH].reshape(3, 3, 3, CH, CH).astype(F32)]
where the time goes in v1:
time: 96.2 us; the launch traced here: 96.1 us
  Pallas kernels  95.4 us (99%)
    pallas_call x1, Pallas kernels, on_device(): pl.pallas_call(functools.partial(kernel, scale), out_shape=(jax.ShapeDtyp...  91 us
    pallas_call x1, Pallas kernels, on_device(): pl.pallas_call(write_out, grid=(steps,), out_shape=(jax.ShapeDtypeStruct(...  4.46 us

profile of v1, /device:TPU:1, one launch (start us, length us, event | category | flops | bytes accessed | tf_op | source)
XLA Modules:
  0.0 96.1 jit_solution(14154897014725207028)
XLA Ops:
  0.6 91.0 %shard_map.75 = (bf16[2,4,256,128]{3,2,1,0:T(8,128)(2,1)}, bf16[2,4,256,128]{3,2,1,0:T(8,128)(2,1)}, bf16[3584,128]{1,0:T(8,128)(2,1)}, bf16[3584,128]{1,0:T(8,128)(2,1)}) custom-call(bf16[2,4,256,128]{3,2,1,0:T(8,128)(2,1)} %clip_in.1, bf16[2,4,256,128]{3,2,1,0:T(8,128)(2,1)} %cotangent_in.1, bf16[27,128,128]{2,1,0:T(8,128)(2,1)} %bitcast.8, ...), custom_call_target="tpu_custom_call" | custom-call | tf_op jit(solution)/shard_map/pallas_call | solution.py:651
  91.6 4.5 %shard_map.76 = (bf16[2048,128]{1,0:T(8,128)(2,1)}, bf16[2048,128]{1,0:T(8,128)(2,1)}, f32[3456,128]{1,0:T(8,128)}, f32[3456,128]{1,0:T(8,128)}) custom-call(bf16[2048,128]{1,0:T(8,128)(2,1)} %bitcast.10, bf16[2048,128]{1,0:T(8,128)(2,1)} %bitcast.11, bf16[3584,128]{1,0:T(8,128)(2,1)} %get-tuple-element.14.first_in, ...), custom_call_target="tpu_custom_call" | custom-call | tf_op jit(solution)/shard_map/pallas_call | solution.py:680

commit v2 on v1

--- a/solution.py
+++ b/solution.py
@@ -261,8 +261,9 @@
         for col in (0, COLS + self.halo):
             self.ref[self.own : self.own + FR, col : col + self.halo] = jnp.zeros((FR, self.halo, ROWN, CH), BF16)
 
-    def put(self, f, value):
-        self.ref[self.own + f, self.halo : self.halo + COLS] = value.astype(BF16).reshape(COLS, ROWN, CH)
+    def put(self, f, start, value):
+        width = value.shape[0] // ROWN
+        self.ref[self.own + f, self.halo + start : self.halo + start + width] = value.astype(BF16).reshape(width, ROWN, CH)
 
     def to_left(self):
         return self.ring.s > 0
@@ -286,29 +287,36 @@
         self.copy(frames, source, to_frames, target, halo, g, s + side, i).start()
 
     def edges(self, q):
-        frames = pl.ds(self.own + 2 * q, 2)
-
-        @pl.when(self.to_left())
-        def _():
-            self.edge(frames, frames, -1, self.ring.g, 2 * q)
-
-        @pl.when(self.to_right())
-        def _():
-            self.edge(frames, frames, 1, self.ring.g, 2 * q + 1)
+        frames, i = self._pair(q)
+
+        @pl.when(self._held(q) & self.to_left())
+        def _():
+            self.edge(frames, frames, -1, self.ring.g, i)
+
+        @pl.when(self._held(q) & self.to_right())
+        def _():
+            self.edge(frames, frames, 1, self.ring.g, i + 1)
+
+    def _pair(self, q):
+        return pl.ds(self.own + 2 * q, 2), (2 * q) % 6
+
+    def _held(self, q):
+        return self.has_source() if q < 0 else self.ring.g >= 0
 
     def await_edges(self, q):
         self._edges(q, self.recv, self.to_right(), self.to_left())
 
     def _edges(self, q, sem, left, right):
-        view = self.ref.at[pl.ds(self.own + 2 * q, 2), pl.ds(0, self.halo)]
-
-        @pl.when(left)
-        def _():
-            pltpu.make_async_copy(view, view, sem.at[2 * q]).wait()
-
-        @pl.when(right)
-        def _():
-            pltpu.make_async_copy(view, view, sem.at[2 * q + 1]).wait()
+        frames, i = self._pair(q)
+        view = self.ref.at[frames, pl.ds(0, self.halo)]
+
+        @pl.when(self._held(q) & left)
+        def _():
+            pltpu.make_async_copy(view, view, sem.at[i]).wait()
+
+        @pl.when(self._held(q) & right)
+        def _():
+            pltpu.make_async_copy(view, view, sem.at[i + 1]).wait()
 
     def span(self):
         return (0, self.width) if self.whole else (self.halo, COLS)
@@ -357,9 +365,10 @@
 
     def finish(self):
         if not self.whole:
-            for q in range(2):
+            for q in range(-1 if self.step > 0 else 0, 2):
                 self._edges(q, self.send, self.to_left(), self.to_right())
-        self._frames(self.send, self.has_target(), self.to_left(), self.to_right())
+        if self.whole or self.step < 0:
+            self._frames(self.send, self.has_target(), self.to_left(), self.to_right())
 
     def slab(self, p, k, start, width):
         return self.ref[2 * p + k, start : start + width].reshape(width * ROWN, CH)
@@ -409,24 +418,36 @@
     return jnp.where(row_index(value.shape) == ROWN - 1, 0.0, pltpu.roll(value, value.shape[0] - 1, axis=0))
 
 
-def convolve(field, weights, p, contract):
-    width = field.width - 2
-    lhs = jnp.concatenate([field.slab(p, k, c, width) for c in range(3) for k in range(4)], axis=1)
+def convolve(field, weights, p, contract, start, width):
+    lhs = jnp.concatenate([field.slab(p, k, start + c, width) for c in range(3) for k in range(4)], axis=1)
     rows = lax.dot_general(lhs, weights[...], (((1,), (contract,)), ((), ())), preferred_element_type=F32)
     above, level, below = (rows[:, b * 2 * CH : (b + 1) * 2 * CH] for b in range(3))
     return level + from_above(above) + from_below(below)
 
 
-def store_turned(turned, delta, p):
+def store_turned(turned, delta, start):
     for b, value in enumerate((from_below(delta), delta, from_above(delta))):
-        turned[b * 2 * CH : (b + 1) * 2 * CH, p * POS : (p + 1) * POS] = value.astype(BF16).T
-
-
-def weight_grads(field, turned, part, scale):
+        turned[b * 2 * CH : (b + 1) * 2 * CH, start : start + delta.shape[0]] = value.astype(BF16).T
+
+
+def pair_sums(field, turned, p, c):
+    rhs = jnp.concatenate([field.slab(p, k, field.halo - 1 + c, COLS) for k in range(4)], axis=1)
+    return lax.dot_general(turned[:, p * POS : (p + 1) * POS], rhs, (((1,), (0,)), ((), ())), preferred_element_type=F32)
+
+
+def begin_grads(field, turned, begun, p):
     for c in range(3):
-        rhs = jnp.concatenate(
-            [jnp.concatenate([field.slab(p, k, field.halo - 1 + c, COLS) for k in range(4)], axis=1) for p in range(2)], axis=0)
-        sums = lax.dot_general(turned[...], rhs, (((1,), (0,)), ((), ())), preferred_element_type=F32)
+        begun[c] = pair_sums(field, turned, p, c)
+
+
+def weight_grads(field, turned, part, scale, begun=None):
+    for c in range(3):
+        if begun is None:
+            rhs = jnp.concatenate(
+                [jnp.concatenate([field.slab(p, k, field.halo - 1 + c, COLS) for k in range(4)], axis=1) for p in range(2)], axis=0)
+            sums = lax.dot_general(turned[...], rhs, (((1,), (0,)), ((), ())), preferred_element_type=F32)
+        else:
+            sums = begun[c] + pair_sums(field, turned, 1, c)
         for b in range(3):
             for a in range(3):
                 one = sums[2 * b * CH : (2 * b + 1) * CH, a * CH : (a + 1) * CH]
@@ -450,16 +471,43 @@
     pltpu.make_async_copy(source.at[:, :, cols], stage.at[pl.ds(2 * ring.y_lo, 2), pl.ds(4 * ring.r, 4)], own).start()
 
 
-def give_back(ring, stage, result, send, recv, own):
+def relay(ring, stage, flat, recv, own, ahead, there, send, landed):
+    for turn in (0, 3, 1, 2):
+        for core in range(2):
+            s = (ring.s + 2 * turn) % GROUP // 2 * 2 + core
+            half, quarter = Ring.parts(s)
+
+            @pl.when(s == ring.s)
+            def _():
+                take(flat, 2 * 4 * COLS, own)
+
+            @pl.when(s != ring.s)
+            def _():
+                take(flat, 2 * 4 * COLS, recv.at[s])
+
+            @pl.when(there & (half == 1))
+            def _():
+                rows = pl.ds(4 * quarter, 4)
+                remote(stage.at[pl.ds(2, 2), rows], ahead.at[:, rows], send, landed, Ring.at(ring.g + 1, ring.s)).start()
+
+
+def give_back(ring, stage, result, send, recv, own, half):
     cols = pl.ds(pl.multiple_of(ring.s * COLS, COLS), COLS)
-
-    @pl.loop(1, GROUP)
-    def _(o):
-        d = (ring.s + o) % GROUP
-        half, quarter = Ring.parts(d)
-        remote(stage.at[pl.ds(2 * half, 2), pl.ds(4 * quarter, 4)], result.at[:, :, cols], send, recv, Ring.at(ring.g, d)).start()
-
-    pltpu.make_async_copy(stage.at[pl.ds(2 * ring.y_lo, 2), pl.ds(4 * ring.r, 4)], result.at[:, :, cols], own).start()
+    pair = pl.ds(2 * half, 2)
+
+    @pl.loop(0, 4)
+    def _(i):
+        quarter = (ring.r + i) % 4
+        rows = pl.ds(4 * quarter, 4)
+        here = (half == ring.y_lo) & (i == 0)
+
+        @pl.when(here)
+        def _():
+            pltpu.make_async_copy(stage.at[pair, rows], result.at[:, :, cols], own).start()
+
+        @pl.when(jnp.logical_not(here))
+        def _():
+            remote(stage.at[pair, rows], result.at[:, :, cols], send, recv, (ring.g * 2 + half, quarter)).start()
 
 
 def await_blocks(flat, sem, own):
@@ -469,8 +517,9 @@
 
 def kernel(scale, clip_in, cotangent_in, first_kernel, second_kernel, critic_map, clip_grad, full_first, full_second,
            clip_a, act_a, second_a, first_a, first_w, first_wt, second_w, second_wt, clip, cotangent, stage, cot_f, slopes,
-           turned, part, other, slots, near, piece, tiles,
-           red_send, red_recv, halo_send, halo_recv, block_send, block_recv, block_own, weight_sem, load_sem):
+           turned, begun, part, other, slots, near, piece, tiles,
+           red_send, red_recv, halo_send, halo_recv, block_send, block_recv, block_own, weight_sem, load_sem,
+           ahead, clip_recv, ahead_sem):
     loads = [pltpu.make_async_copy(source, target, load_sem.at[i])
              for i, (source, target) in enumerate(((clip_in, clip), (cotangent_in, cotangent)))]
     for load in loads:
@@ -513,17 +562,16 @@
     loads[0].wait()
     pl.semaphore_wait(barrier, count)
 
-    spread(ring, clip, stage.at[0], block_send.at[0], block_recv.at[0], block_own.at[0])
-    loads[1].wait()
-    spread(ring, cotangent, stage.at[1], block_send.at[1], block_recv.at[1], block_own.at[1])
+    spread(ring, clip, stage.at[0], block_send.at[0], clip_recv.at[ring.s], block_own.at[0])
     build_weights(second_kernel, second_w, second_wt, weight_sem.at[1])
 
-    await_blocks(full_first, block_recv.at[0], block_own.at[0])
+    relay(ring, stage.at[0], full_first, clip_recv, block_own.at[0], ahead, clips.has_target(), ahead_sem.at[0], ahead_sem.at[1])
     for f in range(FR):
         clip_a[2 + f, 2 : COLS + 2] = swap(stage[0, f])
     clips.edges(0)
     clips.edges(1)
-    clips.frames()
+    loads[1].wait()
+    spread(ring, cotangent, stage.at[1], block_send.at[1], block_recv.at[1], block_own.at[1])
     await_weights(first_w, first_wt, weight_sem.at[0])
     await_weights(second_w, second_wt, weight_sem.at[1])
     clips.await_edges(0)
@@ -534,12 +582,16 @@
         return sigma, sigma * (1.0 + z * (1.0 - sigma))
 
     def first_layer(p):
-        pre = convolve(clips, first_w, p, 0)
-        sigma, slope = sigmoid_slope(pre)
-        act = (pre * sigma).astype(BF16)
-        for j in range(2):
-            act_a[2 + 2 * p + j] = act[:, j * CH : (j + 1) * CH].reshape(COLS + 2, ROWN, CH)
-        slopes[p] = slope[ROWN : ROWN + POS]
+        width = COLS // 2 + 1
+        for half in range(2):
+            start = half * width
+            pre = convolve(clips, first_w, p, 0, start, width)
+            sigma, slope = sigmoid_slope(pre)
+            act = (pre * sigma).astype(BF16)
+            for j in range(2):
+                act_a[2 + 2 * p + j, start : start + width] = act[:, j * CH : (j + 1) * CH].reshape(width, ROWN, CH)
+            skip = ROWN if half == 0 else 0
+            slopes[p, half * POS // 2 : (half + 1) * POS // 2] = slope[skip : skip + POS // 2]
         pair, edge = pl.ds(2 + 2 * p, 2), jnp.zeros((2, ROWN, CH), BF16)
 
         @pl.when(ring.s == 0)
@@ -550,76 +602,128 @@
         def _():
             act_a[pair, COLS + 1] = edge
 
+    width = COLS // 2
+
     def second_layer(p):
-        pre = convolve(acts, second_w, p, 0)
-        sigma, slope = sigmoid_slope(pre)
-        critic = pre * sigma
-        delta = slope * jnp.concatenate(
-            [cot_f[2 * p + j].reshape(POS, CH).astype(F32) for j in range(2)], axis=1)
-        for j in range(2):
-            half = slice(j * CH, (j + 1) * CH)
-            stage[2, 2 * p + j] = swap(critic[:, half].astype(BF16).reshape(COLS, ROWN, CH))
-            seconds.put(2 * p + j, delta[:, half])
-        store_turned(turned, delta, p)
+        for start in (0, width):
+            pre = convolve(acts, second_w, p, 0, start, width)
+            sigma, slope = sigmoid_slope(pre)
+            critic = pre * sigma
+            delta = slope * jnp.concatenate(
+                [cot_f[2 * p + j, start : start + width].reshape(width * ROWN, CH).astype(F32) for j in range(2)], axis=1)
+            for j in range(2):
+                half = slice(j * CH, (j + 1) * CH)
+                stage[2, 2 * p + j, :, start : start + width] = swap(critic[:, half].astype(BF16).reshape(width, ROWN, CH))
+                seconds.put(2 * p + j, start, delta[:, half])
+            store_turned(turned, delta, p * POS + start * ROWN)
 
     def back_layer(p):
-        delta = convolve(seconds, second_wt, p, 1) * slopes[p]
-        for j in range(2):
-            firsts.put(2 * p + j, delta[:, j * CH : (j + 1) * CH])
-        store_turned(turned, delta, p)
+        for start in (0, width):
+            rows = slice(start * ROWN, (start + width) * ROWN)
+            delta = convolve(seconds, second_wt, p, 1, start, width) * slopes[p, rows]
+            for j in range(2):
+                firsts.put(2 * p + j, start, delta[:, j * CH : (j + 1) * CH])
+            store_turned(turned, delta, p * POS + start * ROWN)
 
     def input_layer(p):
-        back = convolve(firsts, first_wt, p, 1)
-        for j in range(2):
-            stage[0, 2 * p + j] = swap(back[:, j * CH : (j + 1) * CH].astype(BF16).reshape(COLS, ROWN, CH))
+        for start in (0, width):
+            back = convolve(firsts, first_wt, p, 1, start, width)
+            for j in range(2):
+                stage[0, 2 * p + j, :, start : start + width] = swap(
+                    back[:, j * CH : (j + 1) * CH].astype(BF16).reshape(width, ROWN, CH))
+
+    def give_critic(half):
+        give_back(ring, stage.at[2], critic_map, block_send.at[2], block_recv.at[2], block_own.at[2], half)
+
+    def give_grad(half):
+        give_back(ring, stage.at[0], clip_grad, block_send.at[3], block_recv.at[3], block_own.at[3], half)
 
     first_layer(1)
     acts.frames()
-    clips.await_frames()
-    first_layer(0)
+
+    @pl.when(clips.has_source())
+    def _():
+        take(full_first, 4 * 2 * 4 * COLS, ahead_sem.at[1])
+        for f in range(2):
+            clip_a[f, 2 : COLS + 2] = swap(ahead[f])
+
+    clips.edges(-1)
     await_blocks(full_first, block_recv.at[1], block_own.at[1])
     for f in range(FR):
         cot_f[f] = swap(stage[1, f])
+    clips.await_edges(-1)
+    first_layer(0)
     second_layer(1)
     seconds.edges(1)
+    give_critic(1)
     acts.await_frames()
     second_layer(0)
     seconds.frames()
     seconds.edges(0)
-    give_back(ring, stage.at[2], critic_map, block_send.at[2], block_recv.at[2], block_own.at[2])
+    give_critic(0)
     weight_grads(acts, turned, part.at[1], scale)
     second_sum.scatter_core()
     seconds.await_edges(0)
     seconds.await_edges(1)
     back_layer(0)
-    firsts.frames()
+    second_sum.scatter_far()
     firsts.edges(0)
-    second_sum.scatter_far()
+
+    @pl.when(me.z != 0)
+    def _():
+        firsts.frames()
+
+    begin_grads(clips, turned, begun, 0)
     seconds.await_frames()
     back_layer(1)
     firsts.edges(1)
+    weight_grads(clips, turned, part.at[0], scale, begun)
+    first_sum.scatter_core()
     second_sum.scatter_near()
-    weight_grads(clips, turned, part.at[0], scale)
-    first_sum.scatter_core()
-    second_sum.scatter_z()
-    take(full_first, (GROUP - 1) * 2 * 4 * COLS, block_send.at[0])
     firsts.await_edges(0)
     firsts.await_edges(1)
     first_sum.scatter_far()
+    take(full_first, (GROUP - 1) * 2 * 4 * COLS, block_send.at[0])
+
+    @pl.when(clips.has_target())
+    def _():
+        take(full_first, 4 * 2 * 4 * COLS, ahead_sem.at[0])
+
     input_layer(0)
-    firsts.await_frames()
-    input_layer(1)
+    second_sum.scatter_z()
+    first_sum.scatter_near()
+
+    @pl.when(me.z != NZ - 1)
+    def _():
+        firsts.await_frames()
+        input_layer(1)
+
+    give_grad(0)
+
+    @pl.when(me.z != NZ - 1)
+    def _():
+        give_grad(1)
+
     second_sum.gather_z()
-    first_sum.scatter_near()
-    give_back(ring, stage.at[0], clip_grad, block_send.at[3], block_recv.at[3], block_own.at[3])
+    first_sum.scatter_z()
+
+    @pl.when(me.z == 0)
+    def _():
+        firsts.frames()
+
     second_sum.gather_near()
-    first_sum.scatter_z()
+
+    @pl.when(me.z == NZ - 1)
+    def _():
+        firsts.await_frames()
+        input_layer(1)
+        give_grad(1)
+
     second_sum.gather_far()
     first_sum.gather_z()
     first_sum.gather_near()
+    second_sum.gather_core()
     first_sum.gather_far()
-    second_sum.gather_core()
-    first_sum.gather_core()
     second_sum.finish()
     for field in fields:
         field.finish()
@@ -627,14 +731,28 @@
         take(full_first, (GROUP - 1) * 2 * 4 * COLS, block_send.at[i])
     for i in range(2, 4):
         await_blocks(full_first, block_recv.at[i], block_own.at[i])
+    first_sum.gather_core()
     first_sum.finish()
 
 
-def write_out(critic_in, grad_in, first_in, second_in, critic, grad, first, second):
-    critic[...] = critic_in[...]
-    grad[...] = grad_in[...]
-    first[...] = first_in[...].astype(F32)
-    second[...] = second_in[...].astype(F32)
+def write_out(critic_in, grad_in, first_in, second_in, critic, grad, first, second, wide, sem):
+    half = 27 * CH // 2
+    stores = []
+    for n, (source, target) in enumerate(((first_in, first), (second_in, second))):
+        for h in range(2):
+            i = 2 * n + h
+
+            @pl.loop(0, half // 192)
+            def _(k):
+                wide[i, rows_of(k * 192, 192), :] = source[rows_of(h * half + k * 192, 192), :].astype(F32)
+
+            stores.append(pltpu.make_async_copy(wide.at[i], target.at[pl.ds(h * half, half)], sem.at[i]))
+            stores[-1].start()
+    for n, (source, target) in enumerate(((critic_in, critic), (grad_in, grad))):
+        stores.append(pltpu.make_async_copy(source, target, sem.at[4 + n]))
+        stores[-1].start()
+    for one in stores:
+        one.wait()
 
 
 def on_device(clip, first_kernel, second_kernel, cotangent):
@@ -651,7 +769,7 @@
     results = pl.pallas_call(
         functools.partial(kernel, scale),
         out_shape=(jax.ShapeDtypeStruct(clip.shape, BF16), jax.ShapeDtypeStruct(clip.shape, BF16), total, total),
-        in_specs=[anywhere] * 4,
+        in_specs=[pl.BlockSpec(memory_space=pltpu.HBM)] * 4,
         out_specs=(vmem, vmem, vmem, vmem),
         scratch_shapes=[
             field(2), field(1), field(1), field(1),
@@ -662,6 +780,7 @@
             pltpu.VMEM((FR, COLS, ROWN, CH), BF16),
             pltpu.VMEM((2, POS, 2 * CH), F32),
             pltpu.VMEM((6 * CH, 2 * POS), BF16),
+            pltpu.VMEM((3, 6 * CH, 4 * CH), F32),
             pltpu.VMEM((2, ROWS, CH), BF16),
             pltpu.VMEM((2, HALF, CH), BF16),
             pltpu.VMEM((2, HALF, CH), BF16),
@@ -669,20 +788,21 @@
             pltpu.VMEM((2, BLK, CH), BF16),
             pltpu.VMEM((2, NZ * TILE, CH), BF16),
             dma((2, 8)), dma((2, 8)), dma((4, 7)), dma((4, 7)), dma((4,)), dma((4,)), dma((4,)), dma((2, 2)), dma((2,)),
+            pltpu.VMEM((2, ROWN, COLS, CH), BF16), dma((GROUP,)), dma((2,)),
         ],
-        compiler_params=pltpu.CompilerParams(collective_id=0, has_side_effects=True, vmem_limit_bytes=60 << 20),
-    )(clip, cotangent, first_kernel.reshape(27, CH, CH), second_kernel.reshape(27, CH, CH))
+        compiler_params=pltpu.CompilerParams(collective_id=0, has_side_effects=True, vmem_limit_bytes=38 << 20),
+    )(*(pltpu.with_memory_space_constraint(one, pltpu.HBM) for one in (
+        clip, cotangent, first_kernel.reshape(27, CH, CH), second_kernel.reshape(27, CH, CH))))
     critic_map, clip_grad, first, second = results
 
-    steps = 4
-    maps, grads = (pl.BlockSpec((rows // steps, CH), lambda i: (i, 0)) for rows in (flat[0], 27 * CH))
     whole = jax.ShapeDtypeStruct((27 * CH, CH), F32)
     critic_map, clip_grad, first, second = pl.pallas_call(
         write_out,
-        grid=(steps,),
         out_shape=(jax.ShapeDtypeStruct(flat, BF16), jax.ShapeDtypeStruct(flat, BF16), whole, whole),
-        in_specs=[maps, maps, grads, grads],
-        out_specs=(maps, maps, grads, grads),
+        in_specs=[vmem] * 4,
+        out_specs=(anywhere,) * 4,
+        scratch_shapes=[pltpu.VMEM((4, 27 * CH // 2, CH), F32), dma((6,))],
+        compiler_params=pltpu.CompilerParams(vmem_limit_bytes=10 << 20),
     )(critic_map.reshape(flat), clip_grad.reshape(flat), first, second)
     taps = (3, 3, 3, CH, CH)
     return critic_map.reshape(clip.shape), clip_grad.reshape(clip.shape), first.reshape(taps), second.reshape(taps)

time: 96.2 us -> 81.8 us (0.85)
  Pallas kernels: 95.4 us -> 80.9 us
    pallas_call x1, Pallas kernels: 91 us -> 78.7 us  [on_device(): pl.pallas_call(functools.partial(kernel, scale), out_shape=(jax.ShapeDtyp...]
    pallas_call x1, Pallas kernels: 4.46 us -> 2.28 us  [on_device(): pl.pallas_call(write_out, out_shape=(jax.ShapeDtypeStruct(flat, BF16), ja...]
where the time goes in v2:
time: 81.8 us; the launch traced here: 81.7 us
  Pallas kernels  80.9 us (99%)
    pallas_call x1, Pallas kernels, on_device(): pl.pallas_call(functools.partial(kernel, scale), out_shape=(jax.ShapeDtyp...  78.7 us
    pallas_call x1, Pallas kernels, on_device(): pl.pallas_call(write_out, out_shape=(jax.ShapeDtypeStruct(flat, BF16), ja...  2.28 us

profile of v2, /device:TPU:1, one launch (start us, length us, event | category | flops | bytes accessed | tf_op | source)
XLA Modules:
  0.0 81.7 jit_solution(6636975632087558193)
XLA Ops:
  0.6 78.7 %shard_map.75 = (bf16[2,4,256,128]{3,2,1,0:T(8,128)(2,1)S(1)}, bf16[2,4,256,128]{3,2,1,0:T(8,128)(2,1)S(1)}, bf16[3584,128]{1,0:T(8,128)(2,1)S(1)}, bf16[3584,128]{1,0:T(8,128)(2,1)S(1)}) custom-call(bf16[2,4,256,128]{3,2,1,0:T(8,128)(2,1)} %clip_in.1, bf16[2,4,256,128]{3,2,1,0:T(8,128)(2,1)} %cotangent_in.1, bf16[27,128,128]{2,1,0:T(8,128)(2,1)} %bitcast.10, ...), custom_call_target="tpu_custom_call" | custom-call | tf_op jit(solution)/shard_map/pallas_call | solution.py:769
  79.3 2.3 %shard_map.76 = (bf16[2048,128]{1,0:T(8,128)(2,1)}, bf16[2048,128]{1,0:T(8,128)(2,1)}, f32[3456,128]{1,0:T(8,128)}, f32[3456,128]{1,0:T(8,128)}) custom-call(bf16[2048,128]{1,0:T(8,128)(2,1)S(1)} %bitcast.8, bf16[2048,128]{1,0:T(8,128)(2,1)S(1)} %bitcast.9, bf16[3584,128]{1,0:T(8,128)(2,1)S(1)} %get-tuple-element.14.first_in, ...), custom_call_target="tpu_custom_call" | custom-call | tf_op jit(solution)/shard_map/pallas_call | solution.py:799

commit v3 on v2

--- a/solution.py
+++ b/solution.py
@@ -461,9 +461,9 @@
 
 
 def spread(ring, source, stage, send, recv, own):
-    @pl.loop(1, GROUP)
-    def _(o):
-        d = (ring.s + o) % GROUP
+    chip, core = ring.s // 2, ring.s % 2
+    for turn, flip in ((0, 1), (1, 0), (3, 0), (1, 1), (3, 1), (2, 0), (2, 1)):
+        d = (chip + turn) % 4 * 2 + (core + flip) % 2
         cols = pl.ds(pl.multiple_of(d * COLS, COLS), COLS)
         remote(source.at[:, :, cols], stage.at[pl.ds(2 * ring.y_lo, 2), pl.ds(4 * ring.r, 4)], send, recv, Ring.at(ring.g, d)).start()
 
@@ -648,11 +648,11 @@
             clip_a[f, 2 : COLS + 2] = swap(ahead[f])
 
     clips.edges(-1)
+    clips.await_edges(-1)
+    first_layer(0)
     await_blocks(full_first, block_recv.at[1], block_own.at[1])
     for f in range(FR):
         cot_f[f] = swap(stage[1, f])
-    clips.await_edges(-1)
-    first_layer(0)
     second_layer(1)
     seconds.edges(1)
     give_critic(1)
@@ -660,11 +660,11 @@
     second_layer(0)
     seconds.frames()
     seconds.edges(0)
-    give_critic(0)
     weight_grads(acts, turned, part.at[1], scale)
     second_sum.scatter_core()
     seconds.await_edges(0)
     seconds.await_edges(1)
+    give_critic(0)
     back_layer(0)
     second_sum.scatter_far()
     firsts.edges(0)
@@ -675,6 +675,11 @@
 
     begin_grads(clips, turned, begun, 0)
     seconds.await_frames()
+
+    @pl.when(me.z == 0)
+    def _():
+        firsts.frames()
+
     back_layer(1)
     firsts.edges(1)
     weight_grads(clips, turned, part.at[0], scale, begun)
@@ -693,37 +698,20 @@
     second_sum.scatter_z()
     first_sum.scatter_near()
 
-    @pl.when(me.z != NZ - 1)
-    def _():
-        firsts.await_frames()
-        input_layer(1)
-
+    firsts.await_frames()
+    input_layer(1)
     give_grad(0)
-
-    @pl.when(me.z != NZ - 1)
-    def _():
-        give_grad(1)
-
+    give_grad(1)
     second_sum.gather_z()
     first_sum.scatter_z()
 
-    @pl.when(me.z == 0)
-    def _():
-        firsts.frames()
-
     second_sum.gather_near()
 
-    @pl.when(me.z == NZ - 1)
-    def _():
-        firsts.await_frames()
-        input_layer(1)
-        give_grad(1)
-
+    first_sum.gather_z()
     second_sum.gather_far()
-    first_sum.gather_z()
     first_sum.gather_near()
+    first_sum.gather_far()
     second_sum.gather_core()
-    first_sum.gather_far()
     second_sum.finish()
     for field in fields:
         field.finish()

time: 81.8 us -> 85.9 us (1.050)
  Pallas kernels: 80.9 us -> 85 us
    pallas_call x1, Pallas kernels: 78.7 us -> 82.7 us  [on_device(): pl.pallas_call(functools.partial(kernel, scale), out_shape=(jax.ShapeDtyp...]
where the time goes in v3:
time: 85.9 us; the launch traced here: 85.8 us
  Pallas kernels  85 us (99%)
    pallas_call x1, Pallas kernels, on_device(): pl.pallas_call(functools.partial(kernel, scale), out_shape=(jax.ShapeDtyp...  82.7 us
    pallas_call x1, Pallas kernels, on_device(): pl.pallas_call(write_out, out_shape=(jax.ShapeDtypeStruct(flat, BF16), ja...  2.28 us

profile of v3, /device:TPU:1, one launch (start us, length us, event | category | flops | bytes accessed | tf_op | source)
XLA Modules:
  0.0 85.8 jit_solution(6528141530836268316)
XLA Ops:
  0.6 82.7 %shard_map.75 = (bf16[2,4,256,128]{3,2,1,0:T(8,128)(2,1)S(1)}, bf16[2,4,256,128]{3,2,1,0:T(8,128)(2,1)S(1)}, bf16[3584,128]{1,0:T(8,128)(2,1)S(1)}, bf16[3584,128]{1,0:T(8,128)(2,1)S(1)}) custom-call(bf16[2,4,256,128]{3,2,1,0:T(8,128)(2,1)} %clip_in.1, bf16[2,4,256,128]{3,2,1,0:T(8,128)(2,1)} %cotangent_in.1, bf16[27,128,128]{2,1,0:T(8,128)(2,1)} %bitcast.10, ...), custom_call_target="tpu_custom_call" | custom-call | tf_op jit(solution)/shard_map/pallas_call | solution.py:757
  83.3 2.3 %shard_map.76 = (bf16[2048,128]{1,0:T(8,128)(2,1)}, bf16[2048,128]{1,0:T(8,128)(2,1)}, f32[3456,128]{1,0:T(8,128)}, f32[3456,128]{1,0:T(8,128)}) custom-call(bf16[2048,128]{1,0:T(8,128)(2,1)S(1)} %bitcast.8, bf16[2048,128]{1,0:T(8,128)(2,1)S(1)} %bitcast.9, bf16[3584,128]{1,0:T(8,128)(2,1)S(1)} %get-tuple-element.14.first_in, ...), custom_call_target="tpu_custom_call" | custom-call | tf_op jit(solution)/shard_map/pallas_call | solution.py:787

commit v4 on v2

--- a/solution.py
+++ b/solution.py
@@ -461,9 +461,9 @@
 
 
 def spread(ring, source, stage, send, recv, own):
-    @pl.loop(1, GROUP)
-    def _(o):
-        d = (ring.s + o) % GROUP
+    chip, core = ring.s // 2, ring.s % 2
+    for turn, flip in ((0, 1), (1, 0), (3, 0), (1, 1), (3, 1), (2, 0), (2, 1)):
+        d = (chip + turn) % 4 * 2 + (core + flip) % 2
         cols = pl.ds(pl.multiple_of(d * COLS, COLS), COLS)
         remote(source.at[:, :, cols], stage.at[pl.ds(2 * ring.y_lo, 2), pl.ds(4 * ring.r, 4)], send, recv, Ring.at(ring.g, d)).start()
 
@@ -648,11 +648,11 @@
             clip_a[f, 2 : COLS + 2] = swap(ahead[f])
 
     clips.edges(-1)
+    clips.await_edges(-1)
+    first_layer(0)
     await_blocks(full_first, block_recv.at[1], block_own.at[1])
     for f in range(FR):
         cot_f[f] = swap(stage[1, f])
-    clips.await_edges(-1)
-    first_layer(0)
     second_layer(1)
     seconds.edges(1)
     give_critic(1)
@@ -660,11 +660,11 @@
     second_layer(0)
     seconds.frames()
     seconds.edges(0)
-    give_critic(0)
     weight_grads(acts, turned, part.at[1], scale)
     second_sum.scatter_core()
     seconds.await_edges(0)
     seconds.await_edges(1)
+    give_critic(0)
     back_layer(0)
     second_sum.scatter_far()
     firsts.edges(0)
@@ -707,11 +707,15 @@
     second_sum.gather_z()
     first_sum.scatter_z()
 
+
     @pl.when(me.z == 0)
     def _():
         firsts.frames()
 
     second_sum.gather_near()
+    first_sum.gather_z()
+    second_sum.gather_far()
+    first_sum.gather_near()
 
     @pl.when(me.z == NZ - 1)
     def _():
@@ -719,11 +723,8 @@
         input_layer(1)
         give_grad(1)
 
-    second_sum.gather_far()
-    first_sum.gather_z()
-    first_sum.gather_near()
+    first_sum.gather_far()
     second_sum.gather_core()
-    first_sum.gather_far()
     second_sum.finish()
     for field in fields:
         field.finish()

time: 81.8 us -> 81.7 us (level)
  no operation moved by 1% of the time
where the time goes in v4:
time: 81.7 us; the launch traced here: 81.6 us
  Pallas kernels  80.8 us (99%)
    pallas_call x1, Pallas kernels, on_device(): pl.pallas_call(functools.partial(kernel, scale), out_shape=(jax.ShapeDtyp...  78.6 us
    pallas_call x1, Pallas kernels, on_device(): pl.pallas_call(write_out, out_shape=(jax.ShapeDtypeStruct(flat, BF16), ja...  2.28 us

profile of v4, /device:TPU:1, one launch (start us, length us, event | category | flops | bytes accessed | tf_op | source)
XLA Modules:
  0.0 81.6 jit_solution(13443410195705698080)
XLA Ops:
  0.6 78.6 %shard_map.75 = (bf16[2,4,256,128]{3,2,1,0:T(8,128)(2,1)S(1)}, bf16[2,4,256,128]{3,2,1,0:T(8,128)(2,1)S(1)}, bf16[3584,128]{1,0:T(8,128)(2,1)S(1)}, bf16[3584,128]{1,0:T(8,128)(2,1)S(1)}) custom-call(bf16[2,4,256,128]{3,2,1,0:T(8,128)(2,1)} %clip_in.1, bf16[2,4,256,128]{3,2,1,0:T(8,128)(2,1)} %cotangent_in.1, bf16[27,128,128]{2,1,0:T(8,128)(2,1)} %bitcast.10, ...), custom_call_target="tpu_custom_call" | custom-call | tf_op jit(solution)/shard_map/pallas_call | solution.py:770
  79.2 2.3 %shard_map.76 = (bf16[2048,128]{1,0:T(8,128)(2,1)}, bf16[2048,128]{1,0:T(8,128)(2,1)}, f32[3456,128]{1,0:T(8,128)}, f32[3456,128]{1,0:T(8,128)}) custom-call(bf16[2048,128]{1,0:T(8,128)(2,1)S(1)} %bitcast.8, bf16[2048,128]{1,0:T(8,128)(2,1)S(1)} %bitcast.9, bf16[3584,128]{1,0:T(8,128)(2,1)S(1)} %get-tuple-element.14.first_in, ...), custom_call_target="tpu_custom_call" | custom-call | tf_op jit(solution)/shard_map/pallas_call | solution.py:800

commit v5 on v3

--- a/solution.py
+++ b/solution.py
@@ -321,16 +321,18 @@
     def span(self):
         return (0, self.width) if self.whole else (self.halo, COLS)
 
-    def frames(self):
+    def frames(self, quarter=None):
         g, s = self.ring.g + self.step, self.ring.s
         mine, theirs = (pl.ds(FR, 2), pl.ds(0, 2)) if self.step > 0 else (pl.ds(0, 2), pl.ds(FR, 2))
         start, width = self.span()
+        if quarter is not None:
+            start, width = start + quarter * (width // 4), width // 4
 
         @pl.when(self.has_target())
         def _():
             self.copy(mine, start, theirs, start, width, g, s, 4).start()
 
-        if self.whole:
+        if self.whole or quarter:
             return
 
         @pl.when(self.has_target() & self.to_left())
@@ -631,6 +633,11 @@
             for j in range(2):
                 stage[0, 2 * p + j, :, start : start + width] = swap(
                     back[:, j * CH : (j + 1) * CH].astype(BF16).reshape(width, ROWN, CH))
+
+    def cross(quarter):
+        @pl.when(me.z == 0)
+        def _():
+            firsts.frames(quarter)
 
     def give_critic(half):
         give_back(ring, stage.at[2], critic_map, block_send.at[2], block_recv.at[2], block_own.at[2], half)
@@ -675,15 +682,13 @@
 
     begin_grads(clips, turned, begun, 0)
     seconds.await_frames()
-
-    @pl.when(me.z == 0)
-    def _():
-        firsts.frames()
-
+    cross(0)
     back_layer(1)
     firsts.edges(1)
+    cross(1)
     weight_grads(clips, turned, part.at[0], scale, begun)
     first_sum.scatter_core()
+    cross(2)
     second_sum.scatter_near()
     firsts.await_edges(0)
     firsts.await_edges(1)
@@ -695,6 +700,7 @@
         take(full_first, 4 * 2 * 4 * COLS, ahead_sem.at[0])
 
     input_layer(0)
+    cross(3)
     second_sum.scatter_z()
     first_sum.scatter_near()
 
@@ -706,10 +712,10 @@
     first_sum.scatter_z()
 
     second_sum.gather_near()
-
     first_sum.gather_z()
     second_sum.gather_far()
     first_sum.gather_near()
+
     first_sum.gather_far()
     second_sum.gather_core()
     second_sum.finish()

time: 85.9 us -> 84.6 us (0.985)
  Pallas kernels: 85 us -> 83.8 us
    pallas_call x1, Pallas kernels: 82.7 us -> 81.5 us  [on_device(): pl.pallas_call(functools.partial(kernel, scale), out_shape=(jax.ShapeDtyp...]
where the time goes in v5:
time: 84.6 us
  Pallas kernels  83.8 us (99%)
    pallas_call x1, Pallas kernels, on_device(): pl.pallas_call(functools.partial(kernel, scale), out_shape=(jax.ShapeDtyp...  81.5 us
    pallas_call x1, Pallas kernels, on_device(): pl.pallas_call(write_out, out_shape=(jax.ShapeDtypeStruct(flat, BF16), ja...  2.28 us

profile of v5, /device:TPU:1, one launch (start us, length us, event | category | flops | bytes accessed | tf_op | source)
XLA Modules:
  0.0 84.6 jit_solution(13011982829580871962)
XLA Ops:
  0.6 81.5 %shard_map.75 = (bf16[2,4,256,128]{3,2,1,0:T(8,128)(2,1)S(1)}, bf16[2,4,256,128]{3,2,1,0:T(8,128)(2,1)S(1)}, bf16[3584,128]{1,0:T(8,128)(2,1)S(1)}, bf16[3584,128]{1,0:T(8,128)(2,1)S(1)}) custom-call(bf16[2,4,256,128]{3,2,1,0:T(8,128)(2,1)} %clip_in.1, bf16[2,4,256,128]{3,2,1,0:T(8,128)(2,1)} %cotangent_in.1, bf16[27,128,128]{2,1,0:T(8,128)(2,1)} %bitcast.10, ...), custom_call_target="tpu_custom_call" | custom-call | tf_op jit(solution)/shard_map/pallas_call | solution.py:763
  82.1 2.3 %shard_map.76 = (bf16[2048,128]{1,0:T(8,128)(2,1)}, bf16[2048,128]{1,0:T(8,128)(2,1)}, f32[3456,128]{1,0:T(8,128)}, f32[3456,128]{1,0:T(8,128)}) custom-call(bf16[2048,128]{1,0:T(8,128)(2,1)S(1)} %bitcast.8, bf16[2048,128]{1,0:T(8,128)(2,1)S(1)} %bitcast.9, bf16[3584,128]{1,0:T(8,128)(2,1)S(1)} %get-tuple-element.14.first_in, ...), custom_call_target="tpu_custom_call" | custom-call | tf_op jit(solution)/shard_map/pallas_call | solution.py:793

commit v6 on v4

--- a/solution.py
+++ b/solution.py
@@ -257,9 +257,20 @@
 
     def clear(self):
         far = 0 if self.own else FR
-        self.ref[far : far + 2] = jnp.zeros((2, self.width, ROWN, CH), BF16)
-        for col in (0, COLS + self.halo):
-            self.ref[self.own : self.own + FR, col : col + self.halo] = jnp.zeros((FR, self.halo, ROWN, CH), BF16)
+
+        @pl.when(jnp.logical_not(self.has_source()))
+        def _():
+            self.ref[far : far + 2] = jnp.zeros((2, self.width, ROWN, CH), BF16)
+
+        edge = jnp.zeros((FR + 2, self.halo, ROWN, CH), BF16)
+
+        @pl.when(jnp.logical_not(self.to_left()))
+        def _():
+            self.ref[:, 0 : self.halo] = edge
+
+        @pl.when(jnp.logical_not(self.to_right()))
+        def _():
+            self.ref[:, COLS + self.halo :] = edge
 
     def put(self, f, start, value):
         width = value.shape[0] // ROWN
@@ -515,11 +526,11 @@
     take(flat, 2 * 4 * COLS, own)
 
 
-def kernel(scale, clip_in, cotangent_in, first_kernel, second_kernel, critic_map, clip_grad, full_first, full_second,
+def kernel(scale, clip_in, cotangent_in, first_kernel, second_kernel, critic_map, clip_grad, full_first, second_out,
            clip_a, act_a, second_a, first_a, first_w, first_wt, second_w, second_wt, clip, cotangent, stage, cot_f, slopes,
            turned, begun, part, other, slots, near, piece, tiles,
            red_send, red_recv, halo_send, halo_recv, block_send, block_recv, block_own, weight_sem, load_sem,
-           ahead, clip_recv, ahead_sem):
+           ahead, clip_recv, ahead_sem, full_second):
     loads = [pltpu.make_async_copy(source, target, load_sem.at[i])
              for i, (source, target) in enumerate(((clip_in, clip), (cotangent_in, cotangent)))]
     for load in loads:
@@ -726,6 +737,12 @@
     first_sum.gather_far()
     second_sum.gather_core()
     second_sum.finish()
+
+    @pl.loop(0, 27 * CH // 192)
+    def _(k):
+        rows = rows_of(k * 192, 192)
+        second_out[rows, :] = full_second[rows, :].astype(F32)
+
     for field in fields:
         field.finish()
     for i in range(1, 4):
@@ -739,19 +756,20 @@
 def write_out(critic_in, grad_in, first_in, second_in, critic, grad, first, second, wide, sem):
     half = 27 * CH // 2
     stores = []
-    for n, (source, target) in enumerate(((first_in, first), (second_in, second))):
-        for h in range(2):
-            i = 2 * n + h
-
-            @pl.loop(0, half // 192)
-            def _(k):
-                wide[i, rows_of(k * 192, 192), :] = source[rows_of(h * half + k * 192, 192), :].astype(F32)
-
-            stores.append(pltpu.make_async_copy(wide.at[i], target.at[pl.ds(h * half, half)], sem.at[i]))
-            stores[-1].start()
-    for n, (source, target) in enumerate(((critic_in, critic), (grad_in, grad))):
-        stores.append(pltpu.make_async_copy(source, target, sem.at[4 + n]))
+
+    def store(source, target):
+        stores.append(pltpu.make_async_copy(source, target, sem.at[len(stores)]))
         stores[-1].start()
+
+    store(second_in, second)
+    for h in range(2):
+        @pl.loop(0, half // 192)
+        def _(k):
+            wide[h, rows_of(k * 192, 192), :] = first_in[rows_of(h * half + k * 192, 192), :].astype(F32)
+
+        store(wide.at[h], first.at[pl.ds(h * half, half)])
+    store(critic_in, critic)
+    store(grad_in, grad)
     for one in stores:
         one.wait()
 
@@ -769,7 +787,8 @@
 
     results = pl.pallas_call(
         functools.partial(kernel, scale),
-        out_shape=(jax.ShapeDtypeStruct(clip.shape, BF16), jax.ShapeDtypeStruct(clip.shape, BF16), total, total),
+        out_shape=(jax.ShapeDtypeStruct(clip.shape, BF16), jax.ShapeDtypeStruct(clip.shape, BF16), total,
+                   jax.ShapeDtypeStruct((27 * CH, CH), F32)),
         in_specs=[pl.BlockSpec(memory_space=pltpu.HBM)] * 4,
         out_specs=(vmem, vmem, vmem, vmem),
         scratch_shapes=[
@@ -790,6 +809,7 @@
             pltpu.VMEM((2, NZ * TILE, CH), BF16),
             dma((2, 8)), dma((2, 8)), dma((4, 7)), dma((4, 7)), dma((4,)), dma((4,)), dma((4,)), dma((2, 2)), dma((2,)),
             pltpu.VMEM((2, ROWN, COLS, CH), BF16), dma((GROUP,)), dma((2,)),
+            pltpu.VMEM((ROWS, CH), BF16),
         ],
         compiler_params=pltpu.CompilerParams(collective_id=0, has_side_effects=True, vmem_limit_bytes=38 << 20),
     )(*(pltpu.with_memory_space_constraint(one, pltpu.HBM) for one in (
@@ -802,7 +822,7 @@
         out_shape=(jax.ShapeDtypeStruct(flat, BF16), jax.ShapeDtypeStruct(flat, BF16), whole, whole),
         in_specs=[vmem] * 4,
         out_specs=(anywhere,) * 4,
-        scratch_shapes=[pltpu.VMEM((4, 27 * CH // 2, CH), F32), dma((6,))],
+        scratch_shapes=[pltpu.VMEM((2, 27 * CH // 2, CH), F32), dma((5,))],
         compiler_params=pltpu.CompilerParams(vmem_limit_bytes=10 << 20),
     )(critic_map.reshape(flat), clip_grad.reshape(flat), first, second)
     taps = (3, 3, 3, CH, CH)

time: 81.7 us -> 81.6 us (level)
  no operation moved by 1% of the time
where the time goes in v6:
time: 81.6 us
  Pallas kernels  80.8 us (99%)
    pallas_call x1, Pallas kernels, on_device(): pl.pallas_call(functools.partial(kernel, scale), out_shape=(jax.ShapeDtyp...  78.6 us
    pallas_call x1, Pallas kernels, on_device(): pl.pallas_call(write_out, out_shape=(jax.ShapeDtypeStruct(flat, BF16), ja...  2.17 us

profile of v6, /device:TPU:1, one launch (start us, length us, event | category | flops | bytes accessed | tf_op | source)
XLA Modules:
  0.0 81.6 jit_solution(14777289988352485660)
XLA Ops:
  0.6 78.6 %shard_map.75 = (bf16[2,4,256,128]{3,2,1,0:T(8,128)(2,1)S(1)}, bf16[2,4,256,128]{3,2,1,0:T(8,128)(2,1)S(1)}, bf16[3584,128]{1,0:T(8,128)(2,1)S(1)}, f32[3456,128]{1,0:T(8,128)S(1)}) custom-call(bf16[2,4,256,128]{3,2,1,0:T(8,128)(2,1)} %clip_in.1, bf16[2,4,256,128]{3,2,1,0:T(8,128)(2,1)} %cotangent_in.1, bf16[27,128,128]{2,1,0:T(8,128)(2,1)} %bitcast.10, ...), custom_call_target="tpu_custom_call" | custom-call | tf_op jit(solution)/shard_map/pallas_call | solution.py:788
  79.2 2.2 %shard_map.76 = (bf16[2048,128]{1,0:T(8,128)(2,1)}, bf16[2048,128]{1,0:T(8,128)(2,1)}, f32[3456,128]{1,0:T(8,128)}, f32[3456,128]{1,0:T(8,128)}) custom-call(bf16[2048,128]{1,0:T(8,128)(2,1)S(1)} %bitcast.8, bf16[2048,128]{1,0:T(8,128)(2,1)S(1)} %bitcast.9, bf16[3584,128]{1,0:T(8,128)(2,1)S(1)} %get-tuple-element.14.first_in, ...), custom_call_target="tpu_custom_call" | custom-call | tf_op jit(solution)/shard_map/pallas_call | solution.py:820

commit v7 on v6

--- a/solution.py
+++ b/solution.py
@@ -690,10 +690,10 @@
     firsts.edges(1)
     weight_grads(clips, turned, part.at[0], scale, begun)
     first_sum.scatter_core()
-    second_sum.scatter_near()
     firsts.await_edges(0)
     firsts.await_edges(1)
     first_sum.scatter_far()
+    second_sum.scatter_near()
     take(full_first, (GROUP - 1) * 2 * 4 * COLS, block_send.at[0])
 
     @pl.when(clips.has_target())

time: 81.6 us -> 82.8 us (1.015)
  Pallas kernels: 80.8 us -> 81.9 us
    pallas_call x1, Pallas kernels: 78.6 us -> 79.7 us  [on_device(): pl.pallas_call(functools.partial(kernel, scale), out_shape=(jax.ShapeDtyp...]
where the time goes in v7:
time: 82.8 us; the launch traced here: 82.7 us
  Pallas kernels  81.9 us (99%)
    pallas_call x1, Pallas kernels, on_device(): pl.pallas_call(functools.partial(kernel, scale), out_shape=(jax.ShapeDtyp...  79.7 us
    pallas_call x1, Pallas kernels, on_device(): pl.pallas_call(write_out, out_shape=(jax.ShapeDtypeStruct(flat, BF16), ja...  2.17 us

profile of v7, /device:TPU:1, one launch (start us, length us, event | category | flops | bytes accessed | tf_op | source)
XLA Modules:
  0.0 82.7 jit_solution(16967952307377084165)
XLA Ops:
  0.6 79.7 %shard_map.75 = (bf16[2,4,256,128]{3,2,1,0:T(8,128)(2,1)S(1)}, bf16[2,4,256,128]{3,2,1,0:T(8,128)(2,1)S(1)}, bf16[3584,128]{1,0:T(8,128)(2,1)S(1)}, f32[3456,128]{1,0:T(8,128)S(1)}) custom-call(bf16[2,4,256,128]{3,2,1,0:T(8,128)(2,1)} %clip_in.1, bf16[2,4,256,128]{3,2,1,0:T(8,128)(2,1)} %cotangent_in.1, bf16[27,128,128]{2,1,0:T(8,128)(2,1)} %bitcast.10, ...), custom_call_target="tpu_custom_call" | custom-call | tf_op jit(solution)/shard_map/pallas_call | solution.py:788
  80.4 2.2 %shard_map.76 = (bf16[2048,128]{1,0:T(8,128)(2,1)}, bf16[2048,128]{1,0:T(8,128)(2,1)}, f32[3456,128]{1,0:T(8,128)}, f32[3456,128]{1,0:T(8,128)}) custom-call(bf16[2048,128]{1,0:T(8,128)(2,1)S(1)} %bitcast.8, bf16[2048,128]{1,0:T(8,128)(2,1)S(1)} %bitcast.9, bf16[3584,128]{1,0:T(8,128)(2,1)S(1)} %get-tuple-element.14.first_in, ...), custom_call_target="tpu_custom_call" | custom-call | tf_op jit(solution)/shard_map/pallas_call | solution.py:820
